TPU v7x, 256 devices: a whole 4x4x8 slice. The times are simulated.
256 devices in a mesh: patch: 64 (over z, y, core), sub: 4 (over x).
Axes of the slice: x: 4, y: 4, z: 8, core: 2. Of those that a mesh axis runs over, the one named last changes fastest.
Arguments:
- sources: int32 [128, 16], replicated, may hold values from 0 to 131071
- diag_coef: float32 [131072], P(('patch', 'sub')), may hold values from 1 to 2
- tiles: float32 [1024, 6, 128, 128], P(('patch', 'sub')), may hold values from -0.109375 to 0.109375
- tile_cols: int32 [1024, 6], P(('patch', 'sub')), may hold values from 0 to 7
- send_rows: int32 [256, 4, 128], P(('patch', 'sub')), may hold values from 0 to 511
- recv_rows: int32 [256, 512], P(('patch', 'sub')), may hold values from 0 to 511, each once within a row
- bounds: float32 [2], replicated, may hold values from 0.3 to 3.2, as said below
Outputs:
- solution: float32 [131072, 128], P(('patch', 'sub'))
- res_norm: float32 [128], replicated
Inputs may be any that keep to these rules, and one draw needn't show every extreme that they name: bounds[0] lies in 0.3 to 0.5 and bounds[1] in 2.6 to 3.2.
All inputs are finite; a program needn't handle non-finite values.
Results may differ from a plain program's by a relative error of at most 0.0001.
Values sent between devices are 32-bit elements; how exact they have to be, the bound alone decides.
A program may use at most 64 MiB of HBM per device.

v0:
```python
import functools

import jax
import jax.numpy as jnp
from jax import lax
from jax.experimental import pallas as pl
from jax.experimental.pallas import tpu as pltpu
from jax.sharding import PartitionSpec as P

MESH = pl.DeviceIdType.MESH
ITERS = 8
GROUPS = 2
PLANES = 8
CUT = 256

NT = (((1,), (1,)), ((), ()))


def dot(a, b):
    return jnp.dot(a, b, preferred_element_type=jnp.float32)


def dot_nt(a, b):
    return lax.dot_general(a, b, NT, preferred_element_type=jnp.float32)


def split(value):
    high = value.astype(jnp.bfloat16)
    low = (value - high.astype(jnp.float32)).astype(jnp.bfloat16)
    return high, low


def one_hot(equal):
    return jnp.where(equal, 1.0, 0.0).astype(jnp.bfloat16)


def kernel(
    shape,
    src_hbm,
    diag_hbm,
    cols_hbm,
    send_hbm,
    recv_hbm,
    bounds_hbm,
    tiles_hbm,
    x_out,
    norm_out,
    src_lanes,
    diag,
    cols,
    send_rows,
    recv_rows,
    bounds,
    tiles,
    place,
    pick,
    tile_pair,
    w_high,
    w_low,
    ext,
    b_own,
    r_own,
    d_own,
    x_own,
    r_pack,
    d_pack,
    x_pack,
    part,
    coef,
    send_buf,
    recv_buf,
    plane_send,
    plane_recv,
    axis_send,
    axis_recv,
    load_sems,
    send_sem,
    recv_sem,
    norm_sems,
):
    n_patch, n_sub, planes = shape
    f32 = jnp.float32
    k_all, rows = b_own.shape
    per_row = tiles.shape[1]
    blk_rows = tiles.shape[0]
    tile = tiles.shape[2]
    n_blocks = place.shape[0]
    halo_blocks = n_blocks - blk_rows
    dirs = 4
    groups = send_sem.shape[1]
    k_group = k_all // groups

    p = lax.axis_index("patch")
    s = lax.axis_index("sub")
    plane = n_patch // planes
    in_plane = plane * n_sub
    my_plane = lax.div(p, plane)
    my_patch = lax.rem(p, plane)
    my_slot = my_patch * n_sub + s

    p_next = lax.rem(p + 1, n_patch)
    p_prev = lax.rem(p + n_patch - 1, n_patch)
    s_next = lax.rem(s + 1, n_sub)
    s_prev = lax.rem(s + n_sub - 1, n_sub)
    targets = ((p_prev, s), (p_next, s), (p, s_prev), (p, s_next))
    lands = (1, 0, 3, 2)

    def plane_target(offset):
        slot = lax.rem(my_slot + offset, in_plane)
        return (my_plane * plane + lax.div(slot, n_sub), lax.rem(slot, n_sub))

    def axis_target(offset):
        return (lax.rem(my_plane + offset, planes) * plane + my_patch, s)

    loads = [
        pltpu.make_async_copy(source, target, load_sems.at[i])
        for i, (source, target) in enumerate(
            (
                (src_hbm, src_lanes),
                (send_hbm, send_rows),
                (bounds_hbm, bounds),
                (recv_hbm, recv_rows),
                (cols_hbm, cols),
                (diag_hbm, diag),
                (tiles_hbm, tiles),
            )
        )
    ]
    for load in loads:
        load.start()
    barrier = pltpu.get_barrier_semaphore()
    greeted = 0
    for target in targets:
        pl.semaphore_signal(barrier, inc=1, device_id=target, device_id_type=MESH)
        greeted += 1
    for offset in range(1, in_plane):
        pl.semaphore_signal(barrier, inc=1, device_id=plane_target(offset), device_id_type=MESH)
        greeted += 1
    for offset in range(1, planes):
        pl.semaphore_signal(barrier, inc=1, device_id=axis_target(offset), device_id_type=MESH)
        greeted += 1

    for load in loads[:3]:
        load.wait()

    lower = jnp.full((8, rows), bounds[0], f32)
    upper = jnp.full((8, rows), bounds[1], f32)
    centre = (lower + upper) / 2.0
    half_width = (upper - lower) / 2.0
    ratio = centre / half_width
    damping = 1.0 / ratio
    for step in range(ITERS - 1):
        following = 1.0 / (2.0 * ratio - damping)
        coef[2 * step] = following * damping
        coef[2 * step + 1] = 2.0 * following / half_width
        damping = following
    inverse = (1.0 / centre)[0:1]

    first = (p * n_sub + s) * rows
    src = jnp.transpose(src_lanes[...])
    lane = lax.broadcasted_iota(jnp.int32, (1, tile), 1) + first
    chunk = 32
    for start in range(0, k_all, chunk):
        ids = [send_rows[j : j + 1, :] + first for j in range(dirs)]
        sums = [jnp.zeros((chunk, tile), f32) for _ in ids]
        for source in range(src.shape[1]):
            wide = jnp.broadcast_to(src[start : start + chunk, source : source + 1], (chunk, tile))
            sums = [jnp.where(wide == v, a + 1.0, a) for v, a in zip(ids, sums)]
        for j, total in enumerate(sums):
            r_pack[start : start + chunk, j * tile : (j + 1) * tile] = total
            scaled = total * inverse[:, :tile]
            d_pack[start : start + chunk, j * tile : (j + 1) * tile] = scaled
            x_pack[start : start + chunk, j * tile : (j + 1) * tile] = scaled
            send_buf[0, j, start : start + chunk, :] = scaled

    pl.semaphore_wait(barrier, greeted)

    def send(step, group, j):
        rows_of = pl.ds(group * k_group, k_group)
        return pltpu.make_async_remote_copy(
            src_ref=send_buf.at[step, j, rows_of, :],
            dst_ref=recv_buf.at[step, lands[j], rows_of, :],
            send_sem=send_sem.at[step, group, j],
            recv_sem=recv_sem.at[step, group, lands[j]],
            device_id=targets[j],
            device_id_type=MESH,
        )

    def start_sends(step, group):
        for j in (2, 3, 0, 1):
            send(step, group, j).start()

    def wait_recvs(step, group):
        for j in (0, 1, 2, 3):
            send(step, group, j).wait_recv()

    def wait_sends(step):
        for group in range(groups):
            for j in range(dirs):
                send(step, group, j).wait_send()

    for group in range(groups):
        start_sends(0, group)

    for start in range(0, k_all, chunk):
        sums = [jnp.zeros((chunk, tile), f32) for _ in range(blk_rows)]
        for source in range(src.shape[1]):
            wide = jnp.broadcast_to(src[start : start + chunk, source : source + 1], (chunk, tile))
            sums = [jnp.where(wide == lane + i * tile, a + 1.0, a) for i, a in enumerate(sums)]
        for i, total in enumerate(sums):
            where = (slice(start, start + chunk), slice(i * tile, (i + 1) * tile))
            b_own[where] = total
            r_own[where] = total
            scaled = total * inverse[:, :tile]
            d_own[where] = scaled
            x_own[where] = scaled
            high, low = split(scaled)
            ext[start : start + chunk, i * tile : (i + 1) * tile] = high
            ext[k_all + start : k_all + start + chunk, i * tile : (i + 1) * tile] = low

    loads[3].wait()

    eye = lax.broadcasted_iota(jnp.int32, (tile, tile), 0) == lax.broadcasted_iota(jnp.int32, (tile, tile), 1)
    row_id = lax.broadcasted_iota(jnp.int32, (rows, tile), 0)
    for c in range(n_blocks):
        if c < blk_rows:
            place[c] = jnp.zeros(place.shape[1:], jnp.bfloat16)
            place[c, c * tile : (c + 1) * tile, :] = one_hot(eye)
        else:
            h = c - blk_rows
            place[c, 0:rows, :] = jnp.zeros((rows, tile), jnp.bfloat16)
            place[c, rows : 2 * rows, :] = one_hot(recv_rows[:, h * tile : (h + 1) * tile] == row_id)
    for j in range(dirs):
        pick[:, j * tile : (j + 1) * tile] = one_hot(send_rows[j : j + 1, :] == row_id)

    for load in loads[4:]:
        load.wait()

    for b in range(blk_rows):
        for n in range(per_row):
            high, low = split(tiles[b, n])
            tile_pair[0:tile, n * tile : (n + 1) * tile] = high
            tile_pair[tile : 2 * tile, n * tile : (n + 1) * tile] = low
        pair = tile_pair[...]
        for start in range(0, 2 * rows, CUT):
            spots = [place[cols[b, n], start : start + CUT, :] for n in range(per_row)]
            both = dot_nt(jnp.concatenate(spots, axis=1), pair)
            block = both[:, :tile] + both[:, tile:]
            offset = b * tile - start
            if 0 <= offset < CUT:
                extra = jnp.where(eye, diag[b : b + 1, :], 0.0)
                pieces = [jnp.zeros((tile, tile), f32)] * (CUT // tile)
                pieces[offset // tile] = extra
                block = block + jnp.concatenate(pieces, axis=0)
            high, low = split(block)
            w_high[start : start + CUT, b * tile : (b + 1) * tile] = high
            w_low[start : start + CUT, b * tile : (b + 1) * tile] = low

    for start in range(0, 2 * rows, CUT):
        for weights in (w_high, w_low):
            weights[start : start + CUT, rows : 2 * rows] = dot(
                weights[start : start + CUT, 0:rows], pick[...]
            ).astype(jnp.bfloat16)

    def product(k_rows, n_cols):
        both = dot(ext[:, k_rows], w_high[k_rows, n_cols])
        return both[:k_all] + both[k_all:] + dot(ext[0:k_all, k_rows], w_low[k_rows, n_cols])

    own, got = slice(0, rows), slice(rows, 2 * rows)

    def packed_part():
        for start in range(0, rows, CUT):
            part[:, start : start + CUT] = product(own, slice(rows + start, rows + start + CUT))

    packed_part()

    def take_halo(step, group):
        at = pl.ds(group * k_group, k_group)
        wait_recvs(step, group)
        halo = jnp.concatenate([recv_buf[step, j, at, :] for j in range(dirs)], axis=1)
        return split(halo)

    def halo_product(high, low, n_cols):
        both = dot(jnp.concatenate([high, low], axis=0), w_high[got, n_cols])
        return both[:k_group] + both[k_group:] + dot(high, w_low[got, n_cols])

    def iteration(step, carry):
        alpha = coef[2 * step][0:1]
        beta = coef[2 * step + 1][0:1]
        last = (step == ITERS - 2).astype(f32)
        for group in range(groups):
            g0 = group * k_group
            at = slice(g0, g0 + k_group)
            high, low = take_halo(step, group)
            ext[at, got] = high
            ext[k_all + g0 : k_all + g0 + k_group, got] = low
            r_new = r_pack[at, :] - (part[at, :] + halo_product(high, low, slice(rows, 2 * rows)))
            d_new = alpha * d_pack[at, :] + beta * r_new
            x_old = x_pack[at, :]
            going = d_new + last * x_old
            for j in range(dirs):
                send_buf[step + 1, j, at, :] = going[:, j * tile : (j + 1) * tile]
            start_sends(step + 1, group)
            r_pack[at, :] = r_new
            d_pack[at, :] = d_new
            x_pack[at, :] = x_old + d_new
        wait_sends(step)
        for start in range(0, rows, CUT):
            at = slice(start, start + CUT)
            r_new = r_own[:, at] - product(slice(0, 2 * rows), at)
            d_new = alpha[:, at] * d_own[:, at] + beta[:, at] * r_new
            r_own[:, at] = r_new
            d_own[:, at] = d_new
        for start in range(0, rows, CUT):
            at = slice(start, start + CUT)
            d_new = d_own[:, at]
            x_old = x_own[:, at]
            x_own[:, at] = x_old + d_new
            high, low = split(d_new + last * x_old)
            ext[0:k_all, at] = high
            ext[k_all : 2 * k_all, at] = low
        packed_part()
        return carry

    lax.fori_loop(0, ITERS - 1, iteration, 0)

    for start in range(0, rows, CUT):
        at = slice(start, start + CUT)
        r_own[:, at] = b_own[:, at] - product(own, at)
    for i in range(blk_rows):
        x_out[i * tile : (i + 1) * tile, :] = jnp.transpose(x_own[:, i * tile : (i + 1) * tile])

    squares = []
    for group in range(groups):
        high, low = take_halo(ITERS - 1, group)
        final = r_own[group * k_group : (group + 1) * k_group, :] - halo_product(high, low, own)
        final = final * final
        total = final[:, 0:tile]
        for i in range(1, blk_rows):
            total = total + final[:, i * tile : (i + 1) * tile]
        squares.append(total)
    squares = jnp.transpose(jnp.concatenate(squares, axis=0))
    mine = jnp.sum(squares, axis=0, keepdims=True)

    plane_send[...] = mine
    plane_recv[my_slot] = mine
    plane_copies = [
        pltpu.make_async_remote_copy(
            src_ref=plane_send,
            dst_ref=plane_recv.at[my_slot],
            send_sem=norm_sems.at[0],
            recv_sem=norm_sems.at[1],
            device_id=plane_target(offset),
            device_id_type=MESH,
        )
        for offset in range(1, in_plane)
    ]
    for copy in plane_copies:
        copy.start()
    others = plane_recv.at[pl.ds(0, in_plane - 1)]
    pltpu.make_async_copy(others, others, norm_sems.at[1]).wait()
    mine = jnp.sum(plane_recv[...], axis=0)

    axis_send[...] = mine
    axis_recv[my_plane] = mine
    axis_copies = [
        pltpu.make_async_remote_copy(
            src_ref=axis_send,
            dst_ref=axis_recv.at[my_plane],
            send_sem=norm_sems.at[2],
            recv_sem=norm_sems.at[3],
            device_id=axis_target(offset),
            device_id_type=MESH,
        )
        for offset in range(1, planes)
    ]
    for copy in axis_copies:
        copy.start()
    wait_sends(ITERS - 1)
    pltpu.make_async_copy(others, others, norm_sems.at[0]).wait()
    others = axis_recv.at[pl.ds(0, planes - 1)]
    pltpu.make_async_copy(others, others, norm_sems.at[3]).wait()
    norm_out[...] = jnp.sqrt(jnp.sum(axis_recv[...], axis=0))
    pltpu.make_async_copy(others, others, norm_sems.at[2]).wait()


def on_device(n_patch, n_sub, planes, sources, diag_coef, tiles, tile_cols, send_rows, recv_rows, bounds):
    rows = diag_coef.shape[0]
    k_all = sources.shape[0]
    blk_rows, per_row, tile, _ = tiles.shape
    dirs = send_rows.shape[1]
    n_blocks = 2 * blk_rows
    f32, bf16 = jnp.float32, jnp.bfloat16
    vmem = pl.BlockSpec(memory_space=pltpu.VMEM)
    hbm = pl.BlockSpec(memory_space=pltpu.HBM)
    field = pltpu.VMEM((k_all, rows), f32)
    in_plane = n_patch // planes * n_sub
    x, norm = pl.pallas_call(
        functools.partial(kernel, (n_patch, n_sub, planes)),
        out_shape=(jax.ShapeDtypeStruct((rows, k_all), f32), jax.ShapeDtypeStruct((1, k_all), f32)),
        in_specs=[hbm] * 7,
        out_specs=(vmem, vmem),
        scratch_shapes=[
            pltpu.VMEM(sources.shape[::-1], jnp.int32),
            pltpu.VMEM((blk_rows, tile), f32),
            pltpu.SMEM(tile_cols.shape, jnp.int32),
            pltpu.VMEM(send_rows.shape[1:], jnp.int32),
            pltpu.VMEM(recv_rows.shape, jnp.int32),
            pltpu.SMEM(bounds.shape, f32),
            pltpu.VMEM(tiles.shape, f32),
            pltpu.VMEM((n_blocks, 2 * rows, tile), bf16),
            pltpu.VMEM((rows, rows), bf16),
            pltpu.VMEM((2 * tile, per_row * tile), bf16),
            pltpu.VMEM((2 * rows, 2 * rows), bf16),
            pltpu.VMEM((2 * rows, 2 * rows), bf16),
            pltpu.VMEM((2 * k_all, 2 * rows), bf16),
            field,
            field,
            field,
            field,
            field,
            field,
            field,
            field,
            pltpu.VMEM((2 * ITERS, 8, rows), f32),
            pltpu.VMEM((ITERS, dirs, k_all, tile), f32),
            pltpu.VMEM((ITERS, dirs, k_all, tile), f32),
            pltpu.VMEM((1, k_all), f32),
            pltpu.VMEM((in_plane, 1, k_all), f32),
            pltpu.VMEM((1, k_all), f32),
            pltpu.VMEM((planes, 1, k_all), f32),
            pltpu.SemaphoreType.DMA((7,)),
            pltpu.SemaphoreType.DMA((ITERS, GROUPS, dirs)),
            pltpu.SemaphoreType.DMA((ITERS, GROUPS, dirs)),
            pltpu.SemaphoreType.DMA((4,)),
        ],
        compiler_params=pltpu.CompilerParams(
            collective_id=0, has_side_effects=True, vmem_limit_bytes=67_043_328
        ),
    )(
        sources.T,
        diag_coef.reshape(blk_rows, tile),
        tile_cols,
        send_rows[0],
        recv_rows,
        bounds,
        tiles,
    )
    return x, norm[0]


def solution(mesh):
    n_patch, n_sub = mesh.shape["patch"], mesh.shape["sub"]
    both = ("patch", "sub")
    return jax.shard_map(
        functools.partial(on_device, n_patch, n_sub, PLANES),
        mesh=mesh,
        in_specs=(
            P(),
            P(both),
            P(both, None, None, None),
            P(both, None),
            P(both, None, None),
            P(both, None),
            P(),
        ),
        out_specs=(P(both, None), P()),
        check_vma=False,
    )
```

profile of v0, /device:TPU:1, one launch (start us, length us, event | category | flops | bytes accessed | tf_op | source)
XLA Modules:
  0.0 59.4 jit_solution(10697060561888893037)
XLA Ops:
  0.6 56.0 %shard_map.86 = (f32[512,128]{1,0:T(8,128)}, f32[1,128]{1,0:T(1,128)}) custom-call(s32[16,128]{1,0:T(8,128)} %bitcast.4, f32[4,128]{1,0:T(4,128)} %bitcast.5, s32[4,6]{1,0:T(4,128)} %cols_hbm.1, s32[4,128]{1,0:T(4,128)} %bitcast.6, s32[1,512]{1,0:T(1,128)} %recv_hbm.1, f32[2]{0:T(128)} %bounds_hbm.1, f32[4,6,128,128]{3,2,1,0:T(8,128)} %tiles_hbm.1), custom_call_target="tpu_custom_call" | custom-call | tf_op jit(solution)/shard_map/pallas_call | solution.py:398
  56.6 1.7 %copy.11 = f32[512,128]{1,0:T(8,128)} copy(f32[512,128]{1,0:T(8,128)} %get-tuple-element.8) | data formatting | bytes 524288
  58.3 1.1 %copy.12 = f32[128]{0:T(128)} copy(f32[128]{0:T(128)} %bitcast.7) | data formatting | bytes 1024
where the time goes:
time: 59.6 us; the launch traced here: 59.4 us
  Pallas kernels  56 us (94%)
  local copies, waits for them, and re-layouts  2.8 us (5%)
  between operations  0.64 us (1%)
    pallas_call x1, Pallas kernels, on_device(): pl.pallas_call(functools.partial(kernel, (n_patch, n_sub, planes)), out_s...  56 us
    unnamed x2, local copies, waits for them, and re-layouts  2.8 us

commit v1 on v0

--- a/solution.py
+++ b/solution.py
@@ -77,6 +77,9 @@
     send_sem,
     recv_sem,
     norm_sems,
+    out_buf,
+    out_sem,
+    hello_sems,
 ):
     n_patch, n_sub, planes = shape
     f32 = jnp.float32
@@ -133,10 +136,7 @@
     for target in targets:
         pl.semaphore_signal(barrier, inc=1, device_id=target, device_id_type=MESH)
         greeted += 1
-    for offset in range(1, in_plane):
-        pl.semaphore_signal(barrier, inc=1, device_id=plane_target(offset), device_id_type=MESH)
-        greeted += 1
-    for offset in range(1, planes):
+    for offset in (1, planes - 1):
         pl.semaphore_signal(barrier, inc=1, device_id=axis_target(offset), device_id_type=MESH)
         greeted += 1
 
@@ -146,14 +146,6 @@
     lower = jnp.full((8, rows), bounds[0], f32)
     upper = jnp.full((8, rows), bounds[1], f32)
     centre = (lower + upper) / 2.0
-    half_width = (upper - lower) / 2.0
-    ratio = centre / half_width
-    damping = 1.0 / ratio
-    for step in range(ITERS - 1):
-        following = 1.0 / (2.0 * ratio - damping)
-        coef[2 * step] = following * damping
-        coef[2 * step + 1] = 2.0 * following / half_width
-        damping = following
     inverse = (1.0 / centre)[0:1]
 
     first = (p * n_sub + s) * rows
@@ -201,6 +193,23 @@
 
     for group in range(groups):
         start_sends(0, group)
+
+    def hello(distance):
+        for offset in (distance, planes - distance):
+            pl.semaphore_signal(
+                hello_sems.at[distance - 1], inc=1, device_id=axis_target(offset), device_id_type=MESH
+            )
+
+    hello(1)
+
+    half_width = (upper - lower) / 2.0
+    ratio = centre / half_width
+    damping = 1.0 / ratio
+    for step in range(ITERS - 1):
+        following = 1.0 / (2.0 * ratio - damping)
+        coef[2 * step] = following * damping
+        coef[2 * step + 1] = 2.0 * following / half_width
+        damping = following
 
     for start in range(0, k_all, chunk):
         sums = [jnp.zeros((chunk, tile), f32) for _ in range(blk_rows)]
@@ -273,6 +282,8 @@
             part[:, start : start + CUT] = product(own, slice(rows + start, rows + start + CUT))
 
     packed_part()
+    pl.semaphore_wait(hello_sems.at[0], 2)
+    hello(2)
 
     def take_halo(step, group):
         at = pl.ds(group * k_group, k_group)
@@ -328,7 +339,11 @@
         at = slice(start, start + CUT)
         r_own[:, at] = b_own[:, at] - product(own, at)
     for i in range(blk_rows):
-        x_out[i * tile : (i + 1) * tile, :] = jnp.transpose(x_own[:, i * tile : (i + 1) * tile])
+        out_buf[i * tile : (i + 1) * tile, :] = jnp.transpose(x_own[:, i * tile : (i + 1) * tile])
+
+    out_copy = pltpu.make_async_copy(out_buf, x_out, out_sem)
+    out_copy.start()
+    pl.semaphore_wait(hello_sems.at[1], 2)
 
     squares = []
     for group in range(groups):
@@ -377,6 +392,7 @@
     for copy in axis_copies:
         copy.start()
     wait_sends(ITERS - 1)
+    out_copy.wait()
     pltpu.make_async_copy(others, others, norm_sems.at[0]).wait()
     others = axis_recv.at[pl.ds(0, planes - 1)]
     pltpu.make_async_copy(others, others, norm_sems.at[3]).wait()
@@ -399,7 +415,7 @@
         functools.partial(kernel, (n_patch, n_sub, planes)),
         out_shape=(jax.ShapeDtypeStruct((rows, k_all), f32), jax.ShapeDtypeStruct((1, k_all), f32)),
         in_specs=[hbm] * 7,
-        out_specs=(vmem, vmem),
+        out_specs=(hbm, vmem),
         scratch_shapes=[
             pltpu.VMEM(sources.shape[::-1], jnp.int32),
             pltpu.VMEM((blk_rows, tile), f32),
@@ -433,6 +449,9 @@
             pltpu.SemaphoreType.DMA((ITERS, GROUPS, dirs)),
             pltpu.SemaphoreType.DMA((ITERS, GROUPS, dirs)),
             pltpu.SemaphoreType.DMA((4,)),
+            pltpu.VMEM((rows, k_all), f32),
+            pltpu.SemaphoreType.DMA,
+            pltpu.SemaphoreType.REGULAR((2,)),
         ],
         compiler_params=pltpu.CompilerParams(
             collective_id=0, has_side_effects=True, vmem_limit_bytes=67_043_328
@@ -446,6 +465,33 @@
         bounds,
         tiles,
     )
+    return settle(x, norm)
+
+
+def settle_kernel(x_in, norm_in, x_out, norm_out, x_buf, norm_buf, sems):
+    steps = ((x_in, x_buf, x_out), (norm_in, norm_buf, norm_out))
+    reads = [pltpu.make_async_copy(a, b, sems.at[i]) for i, (a, b, _) in enumerate(steps)]
+    writes = [pltpu.make_async_copy(b, c, sems.at[2 + i]) for i, (_, b, c) in enumerate(steps)]
+    for read in reads:
+        read.start()
+    for read, write in zip(reads, writes):
+        read.wait()
+        write.start()
+    for write in writes:
+        write.wait()
+
+
+def settle(x, norm):
+    hbm = pl.BlockSpec(memory_space=pl.ANY)
+    arrays = (x, norm)
+    x, norm = pl.pallas_call(
+        settle_kernel,
+        out_shape=tuple(jax.ShapeDtypeStruct(a.shape, a.dtype) for a in arrays),
+        in_specs=[hbm] * 2,
+        out_specs=(hbm, hbm),
+        scratch_shapes=[pltpu.VMEM(a.shape, a.dtype) for a in arrays] + [pltpu.SemaphoreType.DMA((4,))],
+        compiler_params=pltpu.CompilerParams(vmem_limit_bytes=67_043_328),
+    )(x, norm)
     return x, norm[0]
 
 

time: 59.6 us -> 56.9 us (0.955)
  local copies, waits for them, and re-layouts: 2.8 us -> 0 us
    unnamed x2 -> x0, local copies, waits for them, and re-layouts: 2.8 us -> none
    pallas_call x0 -> x1, Pallas kernels: none -> 1.69 us  [settle(): pl.pallas_call(settle_kernel, out_shape=tuple((jax.ShapeDtypeStruct(a.sha...]
    pallas_call x1, Pallas kernels: 56 us -> 54.5 us  [on_device(): pl.pallas_call(functools.partial(kernel, (n_patch, n_sub, planes)), out_s...]
where the time goes in v1:
time: 56.9 us; the launch traced here: 56.8 us
  Pallas kernels  56.1 us (99%)
  between operations  0.64 us (1%)
    pallas_call x1, Pallas kernels, on_device(): pl.pallas_call(functools.partial(kernel, (n_patch, n_sub, planes)), out_s...  54.5 us
    pallas_call x1, Pallas kernels, settle(): pl.pallas_call(settle_kernel, out_shape=tuple((jax.ShapeDtypeStruct(a.sha...  1.69 us

profile of v1, /device:TPU:1, one launch (start us, length us, event | category | flops | bytes accessed | tf_op | source)
XLA Modules:
  0.0 56.8 jit_solution(8260454502493360726)
XLA Ops:
  0.6 54.5 %shard_map.86 = (f32[512,128]{1,0:T(8,128)}, f32[1,128]{1,0:T(1,128)}) custom-call(s32[16,128]{1,0:T(8,128)} %bitcast.4, f32[4,128]{1,0:T(4,128)} %bitcast.5, s32[4,6]{1,0:T(4,128)} %cols_hbm.1, s32[4,128]{1,0:T(4,128)} %bitcast.6, s32[1,512]{1,0:T(1,128)} %recv_hbm.1, f32[2]{0:T(128)} %bounds_hbm.1, f32[4,6,128,128]{3,2,1,0:T(8,128)} %tiles_hbm.1), custom_call_target="tpu_custom_call" | custom-call | tf_op jit(solution)/shard_map/pallas_call | solution.py:414
  55.1 1.7 %shard_map.87 = (f32[512,128]{1,0:T(8,128)}, f32[1,128]{1,0:T(1,128)}) custom-call(f32[512,128]{1,0:T(8,128)} %get-tuple-element.6.x_in, f32[1,128]{1,0:T(1,128)} %get-tuple-element.7.norm_in), custom_call_target="tpu_custom_call" | custom-call | tf_op jit(solution)/shard_map/pallas_call | solution.py:487

commit v2 on v1

--- a/solution.py
+++ b/solution.py
@@ -9,7 +9,7 @@
 
 MESH = pl.DeviceIdType.MESH
 ITERS = 8
-GROUPS = 2
+GROUPS = 4
 PLANES = 8
 CUT = 256
 
@@ -44,7 +44,7 @@
     bounds_hbm,
     tiles_hbm,
     x_out,
-    norm_out,
+    axis_recv,
     src_lanes,
     diag,
     cols,
@@ -72,7 +72,6 @@
     plane_send,
     plane_recv,
     axis_send,
-    axis_recv,
     load_sems,
     send_sem,
     recv_sem,
@@ -172,8 +171,8 @@
         return pltpu.make_async_remote_copy(
             src_ref=send_buf.at[step, j, rows_of, :],
             dst_ref=recv_buf.at[step, lands[j], rows_of, :],
-            send_sem=send_sem.at[step, group, j],
-            recv_sem=recv_sem.at[step, group, lands[j]],
+            send_sem=send_sem.at[lax.rem(step, 2), group],
+            recv_sem=recv_sem.at[lax.rem(step, 2), group],
             device_id=targets[j],
             device_id_type=MESH,
         )
@@ -182,14 +181,16 @@
         for j in (2, 3, 0, 1):
             send(step, group, j).start()
 
+    def wait_all(buf, sems, step, group):
+        parts = buf.at[step, :, pl.ds(group * k_group, k_group), :]
+        pltpu.make_async_copy(parts, parts, sems.at[lax.rem(step, 2), group]).wait()
+
     def wait_recvs(step, group):
-        for j in (0, 1, 2, 3):
-            send(step, group, j).wait_recv()
+        wait_all(recv_buf, recv_sem, step, group)
 
     def wait_sends(step):
         for group in range(groups):
-            for j in range(dirs):
-                send(step, group, j).wait_send()
+            wait_all(send_buf, send_sem, step, group)
 
     for group in range(groups):
         start_sends(0, group)
@@ -377,7 +378,8 @@
     mine = jnp.sum(plane_recv[...], axis=0)
 
     axis_send[...] = mine
-    axis_recv[my_plane] = mine
+    own_copy = pltpu.make_async_copy(axis_send, axis_recv.at[my_plane], norm_sems.at[4])
+    own_copy.start()
     axis_copies = [
         pltpu.make_async_remote_copy(
             src_ref=axis_send,
@@ -396,7 +398,7 @@
     pltpu.make_async_copy(others, others, norm_sems.at[0]).wait()
     others = axis_recv.at[pl.ds(0, planes - 1)]
     pltpu.make_async_copy(others, others, norm_sems.at[3]).wait()
-    norm_out[...] = jnp.sqrt(jnp.sum(axis_recv[...], axis=0))
+    own_copy.wait()
     pltpu.make_async_copy(others, others, norm_sems.at[2]).wait()
 
 
@@ -407,15 +409,14 @@
     dirs = send_rows.shape[1]
     n_blocks = 2 * blk_rows
     f32, bf16 = jnp.float32, jnp.bfloat16
-    vmem = pl.BlockSpec(memory_space=pltpu.VMEM)
     hbm = pl.BlockSpec(memory_space=pltpu.HBM)
     field = pltpu.VMEM((k_all, rows), f32)
     in_plane = n_patch // planes * n_sub
-    x, norm = pl.pallas_call(
+    x, sums = pl.pallas_call(
         functools.partial(kernel, (n_patch, n_sub, planes)),
-        out_shape=(jax.ShapeDtypeStruct((rows, k_all), f32), jax.ShapeDtypeStruct((1, k_all), f32)),
+        out_shape=(jax.ShapeDtypeStruct((rows, k_all), f32), jax.ShapeDtypeStruct((planes, 1, k_all), f32)),
         in_specs=[hbm] * 7,
-        out_specs=(hbm, vmem),
+        out_specs=(hbm, hbm),
         scratch_shapes=[
             pltpu.VMEM(sources.shape[::-1], jnp.int32),
             pltpu.VMEM((blk_rows, tile), f32),
@@ -444,11 +445,10 @@
             pltpu.VMEM((1, k_all), f32),
             pltpu.VMEM((in_plane, 1, k_all), f32),
             pltpu.VMEM((1, k_all), f32),
-            pltpu.VMEM((planes, 1, k_all), f32),
             pltpu.SemaphoreType.DMA((7,)),
-            pltpu.SemaphoreType.DMA((ITERS, GROUPS, dirs)),
-            pltpu.SemaphoreType.DMA((ITERS, GROUPS, dirs)),
-            pltpu.SemaphoreType.DMA((4,)),
+            pltpu.SemaphoreType.DMA((2, GROUPS)),
+            pltpu.SemaphoreType.DMA((2, GROUPS)),
+            pltpu.SemaphoreType.DMA((5,)),
             pltpu.VMEM((rows, k_all), f32),
             pltpu.SemaphoreType.DMA,
             pltpu.SemaphoreType.REGULAR((2,)),
@@ -465,33 +465,41 @@
         bounds,
         tiles,
     )
-    return settle(x, norm)
-
-
-def settle_kernel(x_in, norm_in, x_out, norm_out, x_buf, norm_buf, sems):
-    steps = ((x_in, x_buf, x_out), (norm_in, norm_buf, norm_out))
-    reads = [pltpu.make_async_copy(a, b, sems.at[i]) for i, (a, b, _) in enumerate(steps)]
-    writes = [pltpu.make_async_copy(b, c, sems.at[2 + i]) for i, (_, b, c) in enumerate(steps)]
-    for read in reads:
-        read.start()
-    for read, write in zip(reads, writes):
-        read.wait()
-        write.start()
-    for write in writes:
-        write.wait()
-
-
-def settle(x, norm):
+    return settle(x, sums)
+
+
+def settle_kernel(x_in, sums_in, x_out, norm_out, x_buf, sums_buf, norm_buf, sems):
+    read_sums = pltpu.make_async_copy(sums_in, sums_buf, sems.at[0])
+    read_x = pltpu.make_async_copy(x_in, x_buf, sems.at[1])
+    write_norm = pltpu.make_async_copy(norm_buf, norm_out, sems.at[0])
+    write_x = pltpu.make_async_copy(x_buf, x_out, sems.at[1])
+    read_sums.start()
+    read_x.start()
+    read_sums.wait()
+    norm_buf[...] = jnp.sqrt(jnp.sum(sums_buf[...], axis=0))
+    write_norm.start()
+    read_x.wait()
+    write_x.start()
+    write_norm.wait()
+    write_x.wait()
+
+
+def settle(x, sums):
     hbm = pl.BlockSpec(memory_space=pl.ANY)
-    arrays = (x, norm)
+    norm_shape = jax.ShapeDtypeStruct(sums.shape[1:], sums.dtype)
     x, norm = pl.pallas_call(
         settle_kernel,
-        out_shape=tuple(jax.ShapeDtypeStruct(a.shape, a.dtype) for a in arrays),
+        out_shape=(jax.ShapeDtypeStruct(x.shape, x.dtype), norm_shape),
         in_specs=[hbm] * 2,
         out_specs=(hbm, hbm),
-        scratch_shapes=[pltpu.VMEM(a.shape, a.dtype) for a in arrays] + [pltpu.SemaphoreType.DMA((4,))],
+        scratch_shapes=[
+            pltpu.VMEM(x.shape, x.dtype),
+            pltpu.VMEM(sums.shape, sums.dtype),
+            pltpu.VMEM(norm_shape.shape, norm_shape.dtype),
+            pltpu.SemaphoreType.DMA((2,)),
+        ],
         compiler_params=pltpu.CompilerParams(vmem_limit_bytes=67_043_328),
-    )(x, norm)
+    )(x, sums)
     return x, norm[0]
 
 

time: 56.9 us -> 55 us (0.967)
  Pallas kernels: 56.1 us -> 54.2 us
    pallas_call x1, Pallas kernels: 54.5 us -> 52.5 us  [on_device(): pl.pallas_call(functools.partial(kernel, (n_patch, n_sub, planes)), out_s...]
where the time goes in v2:
time: 55 us; the launch traced here: 54.8 us
  Pallas kernels  54.2 us (99%)
  between operations  0.64 us (1%)
    pallas_call x1, Pallas kernels, on_device(): pl.pallas_call(functools.partial(kernel, (n_patch, n_sub, planes)), out_s...  52.5 us
    pallas_call x1, Pallas kernels, settle(): pl.pallas_call(settle_kernel, out_shape=(jax.ShapeDtypeStruct(x.shape, x....  1.67 us

profile of v2, /device:TPU:1, one launch (start us, length us, event | category | flops | bytes accessed | tf_op | source)
XLA Modules:
  0.0 54.8 jit_solution(13196979019479662310)
XLA Ops:
  0.6 52.5 %shard_map.86 = (f32[512,128]{1,0:T(8,128)}, f32[8,1,128]{2,1,0:T(1,128)}) custom-call(s32[16,128]{1,0:T(8,128)} %bitcast.4, f32[4,128]{1,0:T(4,128)} %bitcast.5, s32[4,6]{1,0:T(4,128)} %cols_hbm.1, s32[4,128]{1,0:T(4,128)} %bitcast.6, s32[1,512]{1,0:T(1,128)} %recv_hbm.1, f32[2]{0:T(128)} %bounds_hbm.1, f32[4,6,128,128]{3,2,1,0:T(8,128)} %tiles_hbm.1), custom_call_target="tpu_custom_call" | custom-call | tf_op jit(solution)/shard_map/pallas_call | solution.py:415
  53.1 1.7 %shard_map.87 = (f32[512,128]{1,0:T(8,128)}, f32[1,128]{1,0:T(1,128)}) custom-call(f32[512,128]{1,0:T(8,128)} %get-tuple-element.6.x_in, f32[8,1,128]{2,1,0:T(1,128)} %get-tuple-element.7.sums_in), custom_call_target="tpu_custom_call" | custom-call | tf_op jit(solution)/shard_map/pallas_call | solution.py:490

commit v3 on v2

--- a/solution.py
+++ b/solution.py
@@ -12,6 +12,8 @@
 GROUPS = 4
 PLANES = 8
 CUT = 256
+BUILD_CUT = 256
+SELECT_CUT = 256
 
 NT = (((1,), (1,)), ((), ()))
 
@@ -139,6 +141,15 @@
         pl.semaphore_signal(barrier, inc=1, device_id=axis_target(offset), device_id_type=MESH)
         greeted += 1
 
+    eye = lax.broadcasted_iota(jnp.int32, (tile, tile), 0) == lax.broadcasted_iota(jnp.int32, (tile, tile), 1)
+    row_id = lax.broadcasted_iota(jnp.int32, (rows, tile), 0)
+    for c in range(n_blocks):
+        if c < blk_rows:
+            place[c] = jnp.zeros(place.shape[1:], jnp.bfloat16)
+            place[c, c * tile : (c + 1) * tile, :] = one_hot(eye)
+        else:
+            place[c, 0:rows, :] = jnp.zeros((rows, tile), jnp.bfloat16)
+
     for load in loads[:3]:
         load.wait()
 
@@ -150,21 +161,13 @@
     first = (p * n_sub + s) * rows
     src = jnp.transpose(src_lanes[...])
     lane = lax.broadcasted_iota(jnp.int32, (1, tile), 1) + first
-    chunk = 32
-    for start in range(0, k_all, chunk):
-        ids = [send_rows[j : j + 1, :] + first for j in range(dirs)]
-        sums = [jnp.zeros((chunk, tile), f32) for _ in ids]
+
+    def count(start, size, ids):
+        sums = [jnp.zeros((size, tile), f32) for _ in ids]
         for source in range(src.shape[1]):
-            wide = jnp.broadcast_to(src[start : start + chunk, source : source + 1], (chunk, tile))
+            wide = jnp.broadcast_to(src[start : start + size, source : source + 1], (size, tile))
             sums = [jnp.where(wide == v, a + 1.0, a) for v, a in zip(ids, sums)]
-        for j, total in enumerate(sums):
-            r_pack[start : start + chunk, j * tile : (j + 1) * tile] = total
-            scaled = total * inverse[:, :tile]
-            d_pack[start : start + chunk, j * tile : (j + 1) * tile] = scaled
-            x_pack[start : start + chunk, j * tile : (j + 1) * tile] = scaled
-            send_buf[0, j, start : start + chunk, :] = scaled
-
-    pl.semaphore_wait(barrier, greeted)
+        return sums
 
     def send(step, group, j):
         rows_of = pl.ds(group * k_group, k_group)
@@ -177,8 +180,8 @@
             device_id_type=MESH,
         )
 
-    def start_sends(step, group):
-        for j in (2, 3, 0, 1):
+    def start_sends(step, group, which=(0, 1, 2, 3)):
+        for j in which:
             send(step, group, j).start()
 
     def wait_all(buf, sems, step, group):
@@ -192,6 +195,63 @@
         for group in range(groups):
             wait_all(send_buf, send_sem, step, group)
 
+    for group in range(groups):
+        at = slice(group * k_group, (group + 1) * k_group)
+        ids = [send_rows[j : j + 1, :] + first for j in range(dirs)]
+        for j, total in enumerate(count(group * k_group, k_group, ids)):
+            scaled = total * inverse[:, :tile]
+            send_buf[0, j, at, :] = scaled
+            r_pack[at, j * tile : (j + 1) * tile] = total
+            d_pack[at, j * tile : (j + 1) * tile] = scaled
+            x_pack[at, j * tile : (j + 1) * tile] = scaled
+
+    loads[3].wait()
+    for c in range(blk_rows, n_blocks):
+        h = c - blk_rows
+        place[c, rows : 2 * rows, :] = one_hot(recv_rows[:, h * tile : (h + 1) * tile] == row_id)
+    for j in range(dirs):
+        pick[:, j * tile : (j + 1) * tile] = one_hot(send_rows[j : j + 1, :] == row_id)
+
+    for load in loads[4:]:
+        load.wait()
+
+    def build_rows(b):
+        for n in range(per_row):
+            high, low = split(tiles[b, n])
+            tile_pair[0:tile, n * tile : (n + 1) * tile] = high
+            tile_pair[tile : 2 * tile, n * tile : (n + 1) * tile] = low
+        pair = tile_pair[...]
+        for start in range(0, 2 * rows, BUILD_CUT):
+            spots = [place[cols[b, n], start : start + BUILD_CUT, :] for n in range(per_row)]
+            both = dot_nt(jnp.concatenate(spots, axis=1), pair)
+            block = both[:, :tile] + both[:, tile:]
+            offset = b * tile - start
+            if 0 <= offset < BUILD_CUT:
+                extra = jnp.where(eye, diag[b : b + 1, :], 0.0)
+                pieces = [jnp.zeros((tile, tile), f32)] * (BUILD_CUT // tile)
+                pieces[offset // tile] = extra
+                block = block + jnp.concatenate(pieces, axis=0)
+            high, low = split(block)
+            w_high[start : start + BUILD_CUT, b * tile : (b + 1) * tile] = high
+            w_low[start : start + BUILD_CUT, b * tile : (b + 1) * tile] = low
+
+        share = k_all // blk_rows
+        at = slice(b * share, (b + 1) * share)
+        low_at = slice(k_all + b * share, k_all + (b + 1) * share)
+        for i, total in enumerate(count(b * share, share, [lane + i * tile for i in range(blk_rows)])):
+            cols_at = slice(i * tile, (i + 1) * tile)
+            b_own[at, cols_at] = total
+            r_own[at, cols_at] = total
+            scaled = total * inverse[:, :tile]
+            d_own[at, cols_at] = scaled
+            x_own[at, cols_at] = scaled
+            high, low = split(scaled)
+            ext[at, cols_at] = high
+            ext[low_at, cols_at] = low
+
+    build_rows(0)
+
+    pl.semaphore_wait(barrier, greeted)
     for group in range(groups):
         start_sends(0, group)
 
@@ -202,6 +262,9 @@
             )
 
     hello(1)
+
+    for b in range(1, blk_rows):
+        build_rows(b)
 
     half_width = (upper - lower) / 2.0
     ratio = centre / half_width
@@ -212,64 +275,10 @@
         coef[2 * step + 1] = 2.0 * following / half_width
         damping = following
 
-    for start in range(0, k_all, chunk):
-        sums = [jnp.zeros((chunk, tile), f32) for _ in range(blk_rows)]
-        for source in range(src.shape[1]):
-            wide = jnp.broadcast_to(src[start : start + chunk, source : source + 1], (chunk, tile))
-            sums = [jnp.where(wide == lane + i * tile, a + 1.0, a) for i, a in enumerate(sums)]
-        for i, total in enumerate(sums):
-            where = (slice(start, start + chunk), slice(i * tile, (i + 1) * tile))
-            b_own[where] = total
-            r_own[where] = total
-            scaled = total * inverse[:, :tile]
-            d_own[where] = scaled
-            x_own[where] = scaled
-            high, low = split(scaled)
-            ext[start : start + chunk, i * tile : (i + 1) * tile] = high
-            ext[k_all + start : k_all + start + chunk, i * tile : (i + 1) * tile] = low
-
-    loads[3].wait()
-
-    eye = lax.broadcasted_iota(jnp.int32, (tile, tile), 0) == lax.broadcasted_iota(jnp.int32, (tile, tile), 1)
-    row_id = lax.broadcasted_iota(jnp.int32, (rows, tile), 0)
-    for c in range(n_blocks):
-        if c < blk_rows:
-            place[c] = jnp.zeros(place.shape[1:], jnp.bfloat16)
-            place[c, c * tile : (c + 1) * tile, :] = one_hot(eye)
-        else:
-            h = c - blk_rows
-            place[c, 0:rows, :] = jnp.zeros((rows, tile), jnp.bfloat16)
-            place[c, rows : 2 * rows, :] = one_hot(recv_rows[:, h * tile : (h + 1) * tile] == row_id)
-    for j in range(dirs):
-        pick[:, j * tile : (j + 1) * tile] = one_hot(send_rows[j : j + 1, :] == row_id)
-
-    for load in loads[4:]:
-        load.wait()
-
-    for b in range(blk_rows):
-        for n in range(per_row):
-            high, low = split(tiles[b, n])
-            tile_pair[0:tile, n * tile : (n + 1) * tile] = high
-            tile_pair[tile : 2 * tile, n * tile : (n + 1) * tile] = low
-        pair = tile_pair[...]
-        for start in range(0, 2 * rows, CUT):
-            spots = [place[cols[b, n], start : start + CUT, :] for n in range(per_row)]
-            both = dot_nt(jnp.concatenate(spots, axis=1), pair)
-            block = both[:, :tile] + both[:, tile:]
-            offset = b * tile - start
-            if 0 <= offset < CUT:
-                extra = jnp.where(eye, diag[b : b + 1, :], 0.0)
-                pieces = [jnp.zeros((tile, tile), f32)] * (CUT // tile)
-                pieces[offset // tile] = extra
-                block = block + jnp.concatenate(pieces, axis=0)
-            high, low = split(block)
-            w_high[start : start + CUT, b * tile : (b + 1) * tile] = high
-            w_low[start : start + CUT, b * tile : (b + 1) * tile] = low
-
-    for start in range(0, 2 * rows, CUT):
+    for start in range(0, 2 * rows, SELECT_CUT):
         for weights in (w_high, w_low):
-            weights[start : start + CUT, rows : 2 * rows] = dot(
-                weights[start : start + CUT, 0:rows], pick[...]
+            weights[start : start + SELECT_CUT, rows : 2 * rows] = dot(
+                weights[start : start + SELECT_CUT, 0:rows], pick[...]
             ).astype(jnp.bfloat16)
 
     def product(k_rows, n_cols):
@@ -306,16 +315,19 @@
             high, low = take_halo(step, group)
             ext[at, got] = high
             ext[k_all + g0 : k_all + g0 + k_group, got] = low
-            r_new = r_pack[at, :] - (part[at, :] + halo_product(high, low, slice(rows, 2 * rows)))
-            d_new = alpha * d_pack[at, :] + beta * r_new
-            x_old = x_pack[at, :]
-            going = d_new + last * x_old
-            for j in range(dirs):
-                send_buf[step + 1, j, at, :] = going[:, j * tile : (j + 1) * tile]
-            start_sends(step + 1, group)
-            r_pack[at, :] = r_new
-            d_pack[at, :] = d_new
-            x_pack[at, :] = x_old + d_new
+            coupled = halo_product(high, low, slice(rows, 2 * rows))
+            for which in ((0, 1), (2, 3)):
+                half = slice(which[0] * tile, (which[-1] + 1) * tile)
+                r_new = r_pack[at, half] - (part[at, half] + coupled[:, half])
+                d_new = alpha[:, half] * d_pack[at, half] + beta[:, half] * r_new
+                x_old = x_pack[at, half]
+                going = d_new + last * x_old
+                for i, j in enumerate(which):
+                    send_buf[step + 1, j, at, :] = going[:, i * tile : (i + 1) * tile]
+                start_sends(step + 1, group, which)
+                r_pack[at, half] = r_new
+                d_pack[at, half] = d_new
+                x_pack[at, half] = x_old + d_new
         wait_sends(step)
         for start in range(0, rows, CUT):
             at = slice(start, start + CUT)

time: 55 us -> 54.4 us (0.989)
  Pallas kernels: 54.2 us -> 53.6 us
    pallas_call x1, Pallas kernels: 52.5 us -> 51.9 us  [on_device(): pl.pallas_call(functools.partial(kernel, (n_patch, n_sub, planes)), out_s...]
where the time goes in v3:
time: 54.4 us; the launch traced here: 54.2 us
  Pallas kernels  53.6 us (99%)
  between operations  0.64 us (1%)
    pallas_call x1, Pallas kernels, on_device(): pl.pallas_call(functools.partial(kernel, (n_patch, n_sub, planes)), out_s...  51.9 us
    pallas_call x1, Pallas kernels, settle(): pl.pallas_call(settle_kernel, out_shape=(jax.ShapeDtypeStruct(x.shape, x....  1.67 us

profile of v3, /device:TPU:1, one launch (start us, length us, event | category | flops | bytes accessed | tf_op | source)
XLA Modules:
  0.0 54.2 jit_solution(10621087357873759454)
XLA Ops:
  0.6 51.9 %shard_map.86 = (f32[512,128]{1,0:T(8,128)}, f32[8,1,128]{2,1,0:T(1,128)}) custom-call(s32[16,128]{1,0:T(8,128)} %bitcast.4, f32[4,128]{1,0:T(4,128)} %bitcast.5, s32[4,6]{1,0:T(4,128)} %cols_hbm.1, s32[4,128]{1,0:T(4,128)} %bitcast.6, s32[1,512]{1,0:T(1,128)} %recv_hbm.1, f32[2]{0:T(128)} %bounds_hbm.1, f32[4,6,128,128]{3,2,1,0:T(8,128)} %tiles_hbm.1), custom_call_target="tpu_custom_call" | custom-call | tf_op jit(solution)/shard_map/pallas_call | solution.py:427
  52.5 1.7 %shard_map.87 = (f32[512,128]{1,0:T(8,128)}, f32[1,128]{1,0:T(1,128)}) custom-call(f32[512,128]{1,0:T(8,128)} %get-tuple-element.6.x_in, f32[8,1,128]{2,1,0:T(1,128)} %get-tuple-element.7.sums_in), custom_call_target="tpu_custom_call" | custom-call | tf_op jit(solution)/shard_map/pallas_call | solution.py:502

commit v4 on v3

--- a/solution.py
+++ b/solution.py
@@ -12,19 +12,6 @@
 GROUPS = 4
 PLANES = 8
 CUT = 256
-BUILD_CUT = 256
-SELECT_CUT = 256
-
-NT = (((1,), (1,)), ((), ()))
-
-
-def dot(a, b):
-    return jnp.dot(a, b, preferred_element_type=jnp.float32)
-
-
-def dot_nt(a, b):
-    return lax.dot_general(a, b, NT, preferred_element_type=jnp.float32)
-
 
 def split(value):
     high = value.astype(jnp.bfloat16)
@@ -36,7 +23,8 @@
     return jnp.where(equal, 1.0, 0.0).astype(jnp.bfloat16)
 
 
-def kernel(
+def steps(
+    accs,
     shape,
     src_hbm,
     diag_hbm,
@@ -83,6 +71,16 @@
     hello_sems,
 ):
     n_patch, n_sub, planes = shape
+    units = range(len(accs))
+    build_accs = [unit_accs[0:2] for unit_accs in accs]
+    field_accs = [unit_accs[2:4] for unit_accs in accs]
+    halo_accs = [unit_accs[4:6] for unit_accs in accs]
+
+    def feed(unit, weights, jobs, transpose=False):
+        pltpu.matmul_push_rhs(weights, staging_register=0, mxu_index=unit, transpose=transpose)
+        for i, (acc, operand) in enumerate(jobs):
+            pltpu.matmul_acc_lhs(acc, operand, load_staged_rhs=0 if i == 0 else None)
+
     f32 = jnp.float32
     k_all, rows = b_own.shape
     per_row = tiles.shape[1]
@@ -220,20 +218,28 @@
             high, low = split(tiles[b, n])
             tile_pair[0:tile, n * tile : (n + 1) * tile] = high
             tile_pair[tile : 2 * tile, n * tile : (n + 1) * tile] = low
-        pair = tile_pair[...]
-        for start in range(0, 2 * rows, BUILD_CUT):
-            spots = [place[cols[b, n], start : start + BUILD_CUT, :] for n in range(per_row)]
-            both = dot_nt(jnp.concatenate(spots, axis=1), pair)
-            block = both[:, :tile] + both[:, tile:]
-            offset = b * tile - start
-            if 0 <= offset < BUILD_CUT:
-                extra = jnp.where(eye, diag[b : b + 1, :], 0.0)
-                pieces = [jnp.zeros((tile, tile), f32)] * (BUILD_CUT // tile)
-                pieces[offset // tile] = extra
-                block = block + jnp.concatenate(pieces, axis=0)
-            high, low = split(block)
-            w_high[start : start + BUILD_CUT, b * tile : (b + 1) * tile] = high
-            w_low[start : start + BUILD_CUT, b * tile : (b + 1) * tile] = low
+        starts = [[(u + len(units) * i) * CUT for i in range(2)] for u in units]
+        for depth in range(0, per_row * tile, CUT):
+            for u in units:
+                jobs = []
+                for acc, start in zip(build_accs[u], starts[u]):
+                    spots = [place[cols[b, n], start : start + CUT, :] for n in range(depth // tile, (depth + CUT) // tile)]
+                    jobs.append((acc, jnp.concatenate(spots, axis=1)))
+                feed(u, tile_pair[:, depth : depth + CUT], jobs, transpose=True)
+        for i in range(2):
+            for u in units:
+                start = starts[u][i]
+                both = pltpu.matmul_pop(build_accs[u][i])
+                block = both[:, :tile] + both[:, tile:]
+                offset = b * tile - start
+                if 0 <= offset < CUT:
+                    extra = jnp.where(eye, diag[b : b + 1, :], 0.0)
+                    pieces = [jnp.zeros((tile, tile), f32)] * (CUT // tile)
+                    pieces[offset // tile] = extra
+                    block = block + jnp.concatenate(pieces, axis=0)
+                high, low = split(block)
+                w_high[start : start + CUT, b * tile : (b + 1) * tile] = high
+                w_low[start : start + CUT, b * tile : (b + 1) * tile] = low
 
         share = k_all // blk_rows
         at = slice(b * share, (b + 1) * share)
@@ -275,21 +281,34 @@
         coef[2 * step + 1] = 2.0 * following / half_width
         damping = following
 
-    for start in range(0, 2 * rows, SELECT_CUT):
-        for weights in (w_high, w_low):
-            weights[start : start + SELECT_CUT, rows : 2 * rows] = dot(
-                weights[start : start + SELECT_CUT, 0:rows], pick[...]
-            ).astype(jnp.bfloat16)
-
-    def product(k_rows, n_cols):
-        both = dot(ext[:, k_rows], w_high[k_rows, n_cols])
-        return both[:k_all] + both[k_all:] + dot(ext[0:k_all, k_rows], w_low[k_rows, n_cols])
+    for start in range(0, 2 * rows, CUT):
+        chunk_rows = slice(start, start + CUT)
+        for depth in range(0, rows, CUT):
+            for u in units:
+                jobs = [(acc, w[chunk_rows, depth : depth + CUT]) for acc, w in zip(build_accs[u], (w_high, w_low))]
+                feed(u, pick[depth : depth + CUT, u * CUT : (u + 1) * CUT], jobs)
+        for i, w in enumerate((w_high, w_low)):
+            for u in units:
+                at = slice(rows + u * CUT, rows + (u + 1) * CUT)
+                w[chunk_rows, at] = pltpu.matmul_pop(build_accs[u][i]).astype(jnp.bfloat16)
 
     own, got = slice(0, rows), slice(rows, 2 * rows)
 
+    def products(depth_all, first_col):
+        for depth in range(0, depth_all, CUT):
+            at = slice(depth, depth + CUT)
+            for weights, lows in ((w_high, True), (w_low, False)):
+                for u in units:
+                    top, bottom = field_accs[u]
+                    jobs = [(top, ext[0:k_all, at])]
+                    if lows:
+                        jobs.append((bottom, ext[k_all : 2 * k_all, at]))
+                    feed(u, weights[at, first_col + u * CUT : first_col + (u + 1) * CUT], jobs)
+        return [pltpu.matmul_pop(top) + pltpu.matmul_pop(bottom) for top, bottom in field_accs]
+
     def packed_part():
-        for start in range(0, rows, CUT):
-            part[:, start : start + CUT] = product(own, slice(rows + start, rows + start + CUT))
+        for u, product in enumerate(products(rows, rows)):
+            part[:, u * CUT : (u + 1) * CUT] = product
 
     packed_part()
     pl.semaphore_wait(hello_sems.at[0], 2)
@@ -301,21 +320,39 @@
         halo = jnp.concatenate([recv_buf[step, j, at, :] for j in range(dirs)], axis=1)
         return split(halo)
 
-    def halo_product(high, low, n_cols):
-        both = dot(jnp.concatenate([high, low], axis=0), w_high[got, n_cols])
-        return both[:k_group] + both[k_group:] + dot(high, w_low[got, n_cols])
+    depths = range(0, rows, CUT)
+
+    def stage(weights, first_col, unit, i):
+        tile_rows = slice(rows + depths[i], rows + depths[i] + CUT)
+        tile_cols = slice(first_col + unit * CUT, first_col + (unit + 1) * CUT)
+        pltpu.matmul_push_rhs(weights[tile_rows, tile_cols], staging_register=i, mxu_index=unit)
+
+    def stage_first(first_col):
+        for i in range(len(depths)):
+            for unit in units:
+                stage(w_high, first_col, unit, i)
+
+    def multiply(high, low, first_col, slot, more):
+        parts = jnp.concatenate([high, low], axis=0)
+        for following in (w_low, w_high if more else None):
+            for i, depth in enumerate(depths):
+                for unit in units:
+                    pltpu.matmul_acc_lhs(halo_accs[unit][slot], parts[:, depth : depth + CUT], load_staged_rhs=i)
+                    if following is not None:
+                        stage(following, first_col, unit, i)
+
+    def collect(slot):
+        both = jnp.concatenate([pltpu.matmul_pop(halo_accs[unit][slot]) for unit in units], axis=1)
+        return both[:k_group] + both[k_group:]
 
     def iteration(step, carry):
         alpha = coef[2 * step][0:1]
         beta = coef[2 * step + 1][0:1]
         last = (step == ITERS - 2).astype(f32)
-        for group in range(groups):
-            g0 = group * k_group
-            at = slice(g0, g0 + k_group)
-            high, low = take_halo(step, group)
-            ext[at, got] = high
-            ext[k_all + g0 : k_all + g0 + k_group, got] = low
-            coupled = halo_product(high, low, slice(rows, 2 * rows))
+
+        def finish(group):
+            at = slice(group * k_group, (group + 1) * k_group)
+            coupled = collect(group % 2)
             for which in ((0, 1), (2, 3)):
                 half = slice(which[0] * tile, (which[-1] + 1) * tile)
                 r_new = r_pack[at, half] - (part[at, half] + coupled[:, half])
@@ -328,10 +365,21 @@
                 r_pack[at, half] = r_new
                 d_pack[at, half] = d_new
                 x_pack[at, half] = x_old + d_new
+
+        stage_first(rows)
+        for group in range(groups):
+            g0 = group * k_group
+            high, low = take_halo(step, group)
+            multiply(high, low, rows, group % 2, group + 1 < groups)
+            ext[g0 : g0 + k_group, got] = high
+            ext[k_all + g0 : k_all + g0 + k_group, got] = low
+            if group > 0:
+                finish(group - 1)
+        finish(groups - 1)
         wait_sends(step)
-        for start in range(0, rows, CUT):
-            at = slice(start, start + CUT)
-            r_new = r_own[:, at] - product(slice(0, 2 * rows), at)
+        for u, product in enumerate(products(2 * rows, 0)):
+            at = slice(u * CUT, (u + 1) * CUT)
+            r_new = r_own[:, at] - product
             d_new = alpha[:, at] * d_own[:, at] + beta[:, at] * r_new
             r_own[:, at] = r_new
             d_own[:, at] = d_new
@@ -348,9 +396,9 @@
 
     lax.fori_loop(0, ITERS - 1, iteration, 0)
 
-    for start in range(0, rows, CUT):
-        at = slice(start, start + CUT)
-        r_own[:, at] = b_own[:, at] - product(own, at)
+    for u, product in enumerate(products(rows, 0)):
+        at = slice(u * CUT, (u + 1) * CUT)
+        r_own[:, at] = b_own[:, at] - product
     for i in range(blk_rows):
         out_buf[i * tile : (i + 1) * tile, :] = jnp.transpose(x_own[:, i * tile : (i + 1) * tile])
 
@@ -358,15 +406,22 @@
     out_copy.start()
     pl.semaphore_wait(hello_sems.at[1], 2)
 
-    squares = []
-    for group in range(groups):
-        high, low = take_halo(ITERS - 1, group)
-        final = r_own[group * k_group : (group + 1) * k_group, :] - halo_product(high, low, own)
+    def square(group):
+        final = r_own[group * k_group : (group + 1) * k_group, :] - collect(group % 2)
         final = final * final
         total = final[:, 0:tile]
         for i in range(1, blk_rows):
             total = total + final[:, i * tile : (i + 1) * tile]
-        squares.append(total)
+        return total
+
+    squares = []
+    stage_first(0)
+    for group in range(groups):
+        high, low = take_halo(ITERS - 1, group)
+        multiply(high, low, 0, group % 2, group + 1 < groups)
+        if group > 0:
+            squares.append(square(group - 1))
+    squares.append(square(groups - 1))
     squares = jnp.transpose(jnp.concatenate(squares, axis=0))
     mine = jnp.sum(squares, axis=0, keepdims=True)
 
@@ -414,6 +469,18 @@
     pltpu.make_async_copy(others, others, norm_sems.at[2]).wait()
 
 
+def kernel(shape, groups, k_all, rows, *refs):
+    heights = (CUT, CUT, k_all, k_all, 2 * k_all // groups, 2 * k_all // groups)
+    units = rows // CUT
+    specs = [pltpu.ACC(unit)((height, CUT), jnp.float32) for unit in range(units) for height in heights]
+
+    def body(*accs):
+        per_unit = [accs[unit * len(heights) : (unit + 1) * len(heights)] for unit in range(units)]
+        steps(per_unit, shape, *refs)
+
+    pl.run_scoped(body, *specs)
+
+
 def on_device(n_patch, n_sub, planes, sources, diag_coef, tiles, tile_cols, send_rows, recv_rows, bounds):
     rows = diag_coef.shape[0]
     k_all = sources.shape[0]
@@ -425,7 +492,7 @@
     field = pltpu.VMEM((k_all, rows), f32)
     in_plane = n_patch // planes * n_sub
     x, sums = pl.pallas_call(
-        functools.partial(kernel, (n_patch, n_sub, planes)),
+        functools.partial(kernel, (n_patch, n_sub, planes), GROUPS, k_all, rows),
         out_shape=(jax.ShapeDtypeStruct((rows, k_all), f32), jax.ShapeDtypeStruct((planes, 1, k_all), f32)),
         in_specs=[hbm] * 7,
         out_specs=(hbm, hbm),

time: 54.4 us -> 54.2 us (level)
  no operation moved by 1% of the time
where the time goes in v4:
time: 54.2 us; the launch traced here: 54.1 us
  Pallas kernels  53.4 us (99%)
  between operations  0.64 us (1%)
    pallas_call x1, Pallas kernels, on_device(): pl.pallas_call(functools.partial(kernel, (n_patch, n_sub, planes), GROUPS...  51.8 us
    pallas_call x1, Pallas kernels, settle(): pl.pallas_call(settle_kernel, out_shape=(jax.ShapeDtypeStruct(x.shape, x....  1.67 us

profile of v4, /device:TPU:1, one launch (start us, length us, event | category | flops | bytes accessed | tf_op | source)
XLA Modules:
  0.0 54.1 jit_solution(11804912145444850866)
XLA Ops:
  0.6 51.8 %shard_map.86 = (f32[512,128]{1,0:T(8,128)}, f32[8,1,128]{2,1,0:T(1,128)}) custom-call(s32[16,128]{1,0:T(8,128)} %bitcast.4, f32[4,128]{1,0:T(4,128)} %bitcast.5, s32[4,6]{1,0:T(4,128)} %refs_2_.1, s32[4,128]{1,0:T(4,128)} %bitcast.6, s32[1,512]{1,0:T(1,128)} %refs_4_.1, f32[2]{0:T(128)} %refs_5_.1, f32[4,6,128,128]{3,2,1,0:T(8,128)} %refs_6_.1), custom_call_target="tpu_custom_call" | custom-call | tf_op jit(solution)/shard_map/pallas_call | solution.py:494
  52.4 1.7 %shard_map.87 = (f32[512,128]{1,0:T(8,128)}, f32[1,128]{1,0:T(1,128)}) custom-call(f32[512,128]{1,0:T(8,128)} %get-tuple-element.6.x_in, f32[8,1,128]{2,1,0:T(1,128)} %get-tuple-element.7.sums_in), custom_call_target="tpu_custom_call" | custom-call | tf_op jit(solution)/shard_map/pallas_call | solution.py:569

commit v5 on v4

--- a/solution.py
+++ b/solution.py
@@ -74,7 +74,7 @@
     units = range(len(accs))
     build_accs = [unit_accs[0:2] for unit_accs in accs]
     field_accs = [unit_accs[2:4] for unit_accs in accs]
-    halo_accs = [unit_accs[4:6] for unit_accs in accs]
+    halo_accs = [unit_accs[4:8] for unit_accs in accs]
 
     def feed(unit, weights, jobs, transpose=False):
         pltpu.matmul_push_rhs(weights, staging_register=0, mxu_index=unit, transpose=transpose)
@@ -320,29 +320,23 @@
         halo = jnp.concatenate([recv_buf[step, j, at, :] for j in range(dirs)], axis=1)
         return split(halo)
 
-    depths = range(0, rows, CUT)
-
-    def stage(weights, first_col, unit, i):
-        tile_rows = slice(rows + depths[i], rows + depths[i] + CUT)
-        tile_cols = slice(first_col + unit * CUT, first_col + (unit + 1) * CUT)
-        pltpu.matmul_push_rhs(weights[tile_rows, tile_cols], staging_register=i, mxu_index=unit)
-
-    def stage_first(first_col):
-        for i in range(len(depths)):
-            for unit in units:
-                stage(w_high, first_col, unit, i)
-
-    def multiply(high, low, first_col, slot, more):
-        parts = jnp.concatenate([high, low], axis=0)
-        for following in (w_low, w_high if more else None):
-            for i, depth in enumerate(depths):
-                for unit in units:
-                    pltpu.matmul_acc_lhs(halo_accs[unit][slot], parts[:, depth : depth + CUT], load_staged_rhs=i)
-                    if following is not None:
-                        stage(following, first_col, unit, i)
-
-    def collect(slot):
-        both = jnp.concatenate([pltpu.matmul_pop(halo_accs[unit][slot]) for unit in units], axis=1)
+    def stage(first_col, half):
+        for i, weights in enumerate((w_high, w_low)):
+            for u in units:
+                tile_rows = slice(rows + u * CUT, rows + (u + 1) * CUT)
+                tile_cols = slice(first_col + half * CUT, first_col + (half + 1) * CUT)
+                pltpu.matmul_push_rhs(weights[tile_rows, tile_cols], staging_register=i, mxu_index=u)
+
+    def multiply(parts, half, slot):
+        for i in range(2):
+            for u in units:
+                acc = halo_accs[u][2 * slot + half]
+                pltpu.matmul_acc_lhs(acc, parts[:, u * CUT : (u + 1) * CUT], load_staged_rhs=i)
+
+    def collect(half, slot):
+        both = pltpu.matmul_pop(halo_accs[0][2 * slot + half])
+        for u in units[1:]:
+            both = both + pltpu.matmul_pop(halo_accs[u][2 * slot + half])
         return both[:k_group] + both[k_group:]
 
     def iteration(step, carry):
@@ -350,32 +344,37 @@
         beta = coef[2 * step + 1][0:1]
         last = (step == ITERS - 2).astype(f32)
 
-        def finish(group):
+        def finish(group, half):
             at = slice(group * k_group, (group + 1) * k_group)
-            coupled = collect(group % 2)
-            for which in ((0, 1), (2, 3)):
-                half = slice(which[0] * tile, (which[-1] + 1) * tile)
-                r_new = r_pack[at, half] - (part[at, half] + coupled[:, half])
-                d_new = alpha[:, half] * d_pack[at, half] + beta[:, half] * r_new
-                x_old = x_pack[at, half]
-                going = d_new + last * x_old
-                for i, j in enumerate(which):
-                    send_buf[step + 1, j, at, :] = going[:, i * tile : (i + 1) * tile]
-                start_sends(step + 1, group, which)
-                r_pack[at, half] = r_new
-                d_pack[at, half] = d_new
-                x_pack[at, half] = x_old + d_new
-
-        stage_first(rows)
+            lanes = slice(half * CUT, (half + 1) * CUT)
+            r_new = r_pack[at, lanes] - (part[at, lanes] + collect(half, group % 2))
+            d_new = alpha[:, lanes] * d_pack[at, lanes] + beta[:, lanes] * r_new
+            x_old = x_pack[at, lanes]
+            going = d_new + last * x_old
+            which = range(half * CUT // tile, (half + 1) * CUT // tile)
+            for i, j in enumerate(which):
+                send_buf[step + 1, j, at, :] = going[:, i * tile : (i + 1) * tile]
+            start_sends(step + 1, group, which)
+            r_pack[at, lanes] = r_new
+            d_pack[at, lanes] = d_new
+            x_pack[at, lanes] = x_old + d_new
+
+        stage(rows, 0)
         for group in range(groups):
             g0 = group * k_group
             high, low = take_halo(step, group)
-            multiply(high, low, rows, group % 2, group + 1 < groups)
+            parts = jnp.concatenate([high, low], axis=0)
+            multiply(parts, 0, group % 2)
+            stage(rows, 1)
+            multiply(parts, 1, group % 2)
+            finish(group, 0)
+            if group > 0:
+                finish(group - 1, 1)
+            if group + 1 < groups:
+                stage(rows, 0)
             ext[g0 : g0 + k_group, got] = high
             ext[k_all + g0 : k_all + g0 + k_group, got] = low
-            if group > 0:
-                finish(group - 1)
-        finish(groups - 1)
+        finish(groups - 1, 1)
         wait_sends(step)
         for u, product in enumerate(products(2 * rows, 0)):
             at = slice(u * CUT, (u + 1) * CUT)
@@ -407,20 +406,27 @@
     pl.semaphore_wait(hello_sems.at[1], 2)
 
     def square(group):
-        final = r_own[group * k_group : (group + 1) * k_group, :] - collect(group % 2)
-        final = final * final
-        total = final[:, 0:tile]
-        for i in range(1, blk_rows):
-            total = total + final[:, i * tile : (i + 1) * tile]
+        at = slice(group * k_group, (group + 1) * k_group)
+        total = jnp.zeros((k_group, tile), f32)
+        for half in range(2):
+            final = r_own[at, half * CUT : (half + 1) * CUT] - collect(half, group % 2)
+            final = final * final
+            for i in range(CUT // tile):
+                total = total + final[:, i * tile : (i + 1) * tile]
         return total
 
     squares = []
-    stage_first(0)
+    stage(0, 0)
     for group in range(groups):
         high, low = take_halo(ITERS - 1, group)
-        multiply(high, low, 0, group % 2, group + 1 < groups)
+        parts = jnp.concatenate([high, low], axis=0)
+        multiply(parts, 0, group % 2)
+        stage(0, 1)
+        multiply(parts, 1, group % 2)
         if group > 0:
             squares.append(square(group - 1))
+        if group + 1 < groups:
+            stage(0, 0)
     squares.append(square(groups - 1))
     squares = jnp.transpose(jnp.concatenate(squares, axis=0))
     mine = jnp.sum(squares, axis=0, keepdims=True)
@@ -470,7 +476,7 @@
 
 
 def kernel(shape, groups, k_all, rows, *refs):
-    heights = (CUT, CUT, k_all, k_all, 2 * k_all // groups, 2 * k_all // groups)
+    heights = (CUT, CUT, k_all, k_all) + 4 * (2 * k_all // groups,)
     units = rows // CUT
     specs = [pltpu.ACC(unit)((height, CUT), jnp.float32) for unit in range(units) for height in heights]
 

time: 54.2 us -> 53 us (0.978)
  Pallas kernels: 53.4 us -> 52.2 us
    pallas_call x1, Pallas kernels: 51.8 us -> 50.5 us  [on_device(): pl.pallas_call(functools.partial(kernel, (n_patch, n_sub, planes), GROUPS...]
where the time goes in v5:
time: 53 us; the launch traced here: 52.8 us
  Pallas kernels  52.2 us (98%)
  between operations  0.64 us (1%)
    pallas_call x1, Pallas kernels, on_device(): pl.pallas_call(functools.partial(kernel, (n_patch, n_sub, planes), GROUPS...  50.5 us
    pallas_call x1, Pallas kernels, settle(): pl.pallas_call(settle_kernel, out_shape=(jax.ShapeDtypeStruct(x.shape, x....  1.67 us

profile of v5, /device:TPU:1, one launch (start us, length us, event | category | flops | bytes accessed | tf_op | source)
XLA Modules:
  0.0 52.8 jit_solution(2982633079742948584)
XLA Ops:
  0.6 50.5 %shard_map.86 = (f32[512,128]{1,0:T(8,128)}, f32[8,1,128]{2,1,0:T(1,128)}) custom-call(s32[16,128]{1,0:T(8,128)} %bitcast.4, f32[4,128]{1,0:T(4,128)} %bitcast.5, s32[4,6]{1,0:T(4,128)} %refs_2_.1, s32[4,128]{1,0:T(4,128)} %bitcast.6, s32[1,512]{1,0:T(1,128)} %refs_4_.1, f32[2]{0:T(128)} %refs_5_.1, f32[4,6,128,128]{3,2,1,0:T(8,128)} %refs_6_.1), custom_call_target="tpu_custom_call" | custom-call | tf_op jit(solution)/shard_map/pallas_call | solution.py:500
  51.2 1.7 %shard_map.87 = (f32[512,128]{1,0:T(8,128)}, f32[1,128]{1,0:T(1,128)}) custom-call(f32[512,128]{1,0:T(8,128)} %get-tuple-element.6.x_in, f32[8,1,128]{2,1,0:T(1,128)} %get-tuple-element.7.sums_in), custom_call_target="tpu_custom_call" | custom-call | tf_op jit(solution)/shard_map/pallas_call | solution.py:575

commit v6 on v5

--- a/solution.py
+++ b/solution.py
@@ -107,9 +107,16 @@
     targets = ((p_prev, s), (p_next, s), (p, s_prev), (p, s_next))
     lands = (1, 0, 3, 2)
 
-    def plane_target(offset):
-        slot = lax.rem(my_slot + offset, in_plane)
-        return (my_plane * plane + lax.div(slot, n_sub), lax.rem(slot, n_sub))
+    def plane_target(step):
+        patch_step, sub_step = step
+        return (my_plane * plane + lax.rem(my_patch + patch_step, plane), lax.rem(s + sub_step, n_sub))
+
+    def ring(step, size):
+        return min(step, size - step)
+
+    plane_steps = [(a, b) for a in range(plane) for b in range(n_sub) if a or b]
+    plane_steps.sort(key=lambda step: -(ring(step[0], plane) / 2 + ring(step[1], n_sub)))
+    axis_steps = sorted(range(1, planes), key=lambda step: -ring(step, planes))
 
     def axis_target(offset):
         return (lax.rem(my_plane + offset, planes) * plane + my_patch, s)
@@ -367,11 +374,11 @@
             multiply(parts, 0, group % 2)
             stage(rows, 1)
             multiply(parts, 1, group % 2)
+            if group + 1 < groups:
+                stage(rows, 0)
             finish(group, 0)
             if group > 0:
                 finish(group - 1, 1)
-            if group + 1 < groups:
-                stage(rows, 0)
             ext[g0 : g0 + k_group, got] = high
             ext[k_all + g0 : k_all + g0 + k_group, got] = low
         finish(groups - 1, 1)
@@ -439,10 +446,10 @@
             dst_ref=plane_recv.at[my_slot],
             send_sem=norm_sems.at[0],
             recv_sem=norm_sems.at[1],
-            device_id=plane_target(offset),
+            device_id=plane_target(step),
             device_id_type=MESH,
         )
-        for offset in range(1, in_plane)
+        for step in plane_steps
     ]
     for copy in plane_copies:
         copy.start()
@@ -462,7 +469,7 @@
             device_id=axis_target(offset),
             device_id_type=MESH,
         )
-        for offset in range(1, planes)
+        for offset in axis_steps
     ]
     for copy in axis_copies:
         copy.start()

time: 53 us -> 53.1 us (level)
  no operation moved by 1% of the time
where the time goes in v6:
time: 53.1 us; the launch traced here: 53 us
  Pallas kernels  52.3 us (98%)
  between operations  0.64 us (1%)
    pallas_call x1, Pallas kernels, on_device(): pl.pallas_call(functools.partial(kernel, (n_patch, n_sub, planes), GROUPS...  50.6 us
    pallas_call x1, Pallas kernels, settle(): pl.pallas_call(settle_kernel, out_shape=(jax.ShapeDtypeStruct(x.shape, x....  1.67 us

profile of v6, /device:TPU:1, one launch (start us, length us, event | category | flops | bytes accessed | tf_op | source)
XLA Modules:
  0.0 53.0 jit_solution(16630164862932213238)
XLA Ops:
  0.6 50.6 %shard_map.86 = (f32[512,128]{1,0:T(8,128)}, f32[8,1,128]{2,1,0:T(1,128)}) custom-call(s32[16,128]{1,0:T(8,128)} %bitcast.4, f32[4,128]{1,0:T(4,128)} %bitcast.5, s32[4,6]{1,0:T(4,128)} %refs_2_.1, s32[4,128]{1,0:T(4,128)} %bitcast.6, s32[1,512]{1,0:T(1,128)} %refs_4_.1, f32[2]{0:T(128)} %refs_5_.1, f32[4,6,128,128]{3,2,1,0:T(8,128)} %refs_6_.1), custom_call_target="tpu_custom_call" | custom-call | tf_op jit(solution)/shard_map/pallas_call | solution.py:507
  51.3 1.7 %shard_map.87 = (f32[512,128]{1,0:T(8,128)}, f32[1,128]{1,0:T(1,128)}) custom-call(f32[512,128]{1,0:T(8,128)} %get-tuple-element.6.x_in, f32[8,1,128]{2,1,0:T(1,128)} %get-tuple-element.7.sums_in), custom_call_target="tpu_custom_call" | custom-call | tf_op jit(solution)/shard_map/pallas_call | solution.py:582

commit v7 on v6

--- a/solution.py
+++ b/solution.py
@@ -69,6 +69,7 @@
     out_buf,
     out_sem,
     hello_sems,
+    diag_rows,
 ):
     n_patch, n_sub, planes = shape
     units = range(len(accs))
@@ -238,12 +239,6 @@
                 start = starts[u][i]
                 both = pltpu.matmul_pop(build_accs[u][i])
                 block = both[:, :tile] + both[:, tile:]
-                offset = b * tile - start
-                if 0 <= offset < CUT:
-                    extra = jnp.where(eye, diag[b : b + 1, :], 0.0)
-                    pieces = [jnp.zeros((tile, tile), f32)] * (CUT // tile)
-                    pieces[offset // tile] = extra
-                    block = block + jnp.concatenate(pieces, axis=0)
                 high, low = split(block)
                 w_high[start : start + CUT, b * tile : (b + 1) * tile] = high
                 w_low[start : start + CUT, b * tile : (b + 1) * tile] = low
@@ -313,9 +308,26 @@
                     feed(u, weights[at, first_col + u * CUT : first_col + (u + 1) * CUT], jobs)
         return [pltpu.matmul_pop(top) + pltpu.matmul_pop(bottom) for top, bottom in field_accs]
 
+    on_own = jnp.concatenate([diag[b : b + 1, :] for b in range(blk_rows)], axis=1)
+    line = lax.broadcasted_iota(jnp.int32, (2 * k_group, rows), 0)
+    rest, thirds = on_own, jnp.zeros((2 * k_group, rows), f32)
+    for i in range(3):
+        third = rest.astype(jnp.bfloat16).astype(f32)
+        thirds = jnp.where(line == i, third, thirds)
+        rest = rest - third
+    thirds = thirds.astype(jnp.bfloat16)
+    for depth in range(0, rows, CUT):
+        for u in units:
+            jobs = [(halo_accs[u][0], thirds[:, depth : depth + CUT])]
+            feed(u, pick[depth : depth + CUT, u * CUT : (u + 1) * CUT], jobs)
+    on_pack = [jnp.sum(pltpu.matmul_pop(halo_accs[u][0])[0:8], axis=0, keepdims=True) for u in units]
+    diag_rows[0:1, :] = on_own
+    diag_rows[1:2, :] = jnp.concatenate(on_pack, axis=1)
+
     def packed_part():
         for u, product in enumerate(products(rows, rows)):
-            part[:, u * CUT : (u + 1) * CUT] = product
+            at = slice(u * CUT, (u + 1) * CUT)
+            part[:, at] = product + diag_rows[1:2, at] * d_pack[:, at]
 
     packed_part()
     pl.semaphore_wait(hello_sems.at[0], 2)
@@ -385,7 +397,7 @@
         wait_sends(step)
         for u, product in enumerate(products(2 * rows, 0)):
             at = slice(u * CUT, (u + 1) * CUT)
-            r_new = r_own[:, at] - product
+            r_new = r_own[:, at] - (product + diag_rows[0:1, at] * d_own[:, at])
             d_new = alpha[:, at] * d_own[:, at] + beta[:, at] * r_new
             r_own[:, at] = r_new
             d_own[:, at] = d_new
@@ -404,7 +416,7 @@
 
     for u, product in enumerate(products(rows, 0)):
         at = slice(u * CUT, (u + 1) * CUT)
-        r_own[:, at] = b_own[:, at] - product
+        r_own[:, at] = b_own[:, at] - (product + diag_rows[0:1, at] * x_own[:, at])
     for i in range(blk_rows):
         out_buf[i * tile : (i + 1) * tile, :] = jnp.transpose(x_own[:, i * tile : (i + 1) * tile])
 
@@ -544,6 +556,7 @@
             pltpu.VMEM((rows, k_all), f32),
             pltpu.SemaphoreType.DMA,
             pltpu.SemaphoreType.REGULAR((2,)),
+            pltpu.VMEM((8, rows), f32),
         ],
         compiler_params=pltpu.CompilerParams(
             collective_id=0, has_side_effects=True, vmem_limit_bytes=67_043_328

time: 53.1 us -> 53.1 us (level)
  no operation moved by 1% of the time
where the time goes in v7:
time: 53.1 us; the launch traced here: 53 us
  Pallas kernels  52.3 us (98%)
  between operations  0.64 us (1%)
    pallas_call x1, Pallas kernels, on_device(): pl.pallas_call(functools.partial(kernel, (n_patch, n_sub, planes), GROUPS...  50.6 us
    pallas_call x1, Pallas kernels, settle(): pl.pallas_call(settle_kernel, out_shape=(jax.ShapeDtypeStruct(x.shape, x....  1.67 us

profile of v7, /device:TPU:1, one launch (start us, length us, event | category | flops | bytes accessed | tf_op | source)
XLA Modules:
  0.0 53.0 jit_solution(10302326554964286542)
XLA Ops:
  0.6 50.6 %shard_map.86 = (f32[512,128]{1,0:T(8,128)}, f32[8,1,128]{2,1,0:T(1,128)}) custom-call(s32[16,128]{1,0:T(8,128)} %bitcast.4, f32[4,128]{1,0:T(4,128)} %bitcast.5, s32[4,6]{1,0:T(4,128)} %refs_2_.1, s32[4,128]{1,0:T(4,128)} %bitcast.6, s32[1,512]{1,0:T(1,128)} %refs_4_.1, f32[2]{0:T(128)} %refs_5_.1, f32[4,6,128,128]{3,2,1,0:T(8,128)} %refs_6_.1), custom_call_target="tpu_custom_call" | custom-call | tf_op jit(solution)/shard_map/pallas_call | solution.py:519
  51.3 1.7 %shard_map.87 = (f32[512,128]{1,0:T(8,128)}, f32[1,128]{1,0:T(1,128)}) custom-call(f32[512,128]{1,0:T(8,128)} %get-tuple-element.6.x_in, f32[8,1,128]{2,1,0:T(1,128)} %get-tuple-element.7.sums_in), custom_call_target="tpu_custom_call" | custom-call | tf_op jit(solution)/shard_map/pallas_call | solution.py:595

commit v8 on v7

--- a/solution.py
+++ b/solution.py
@@ -62,12 +62,11 @@
     plane_send,
     plane_recv,
     axis_send,
-    load_sems,
+    copy_sems,
     send_sem,
     recv_sem,
     norm_sems,
     out_buf,
-    out_sem,
     hello_sems,
     diag_rows,
 ):
@@ -75,7 +74,7 @@
     units = range(len(accs))
     build_accs = [unit_accs[0:2] for unit_accs in accs]
     field_accs = [unit_accs[2:4] for unit_accs in accs]
-    halo_accs = [unit_accs[4:8] for unit_accs in accs]
+    halo_accs = [unit_accs[4:12] for unit_accs in accs]
 
     def feed(unit, weights, jobs, transpose=False):
         pltpu.matmul_push_rhs(weights, staging_register=0, mxu_index=unit, transpose=transpose)
@@ -90,7 +89,7 @@
     n_blocks = place.shape[0]
     halo_blocks = n_blocks - blk_rows
     dirs = 4
-    groups = send_sem.shape[1]
+    groups = recv_sem.shape[1]
     k_group = k_all // groups
 
     p = lax.axis_index("patch")
@@ -123,7 +122,7 @@
         return (lax.rem(my_plane + offset, planes) * plane + my_patch, s)
 
     loads = [
-        pltpu.make_async_copy(source, target, load_sems.at[i])
+        pltpu.make_async_copy(source, target, copy_sems.at[i])
         for i, (source, target) in enumerate(
             (
                 (src_hbm, src_lanes),
@@ -180,7 +179,7 @@
         return pltpu.make_async_remote_copy(
             src_ref=send_buf.at[step, j, rows_of, :],
             dst_ref=recv_buf.at[step, lands[j], rows_of, :],
-            send_sem=send_sem.at[lax.rem(step, 2), group],
+            send_sem=send_sem.at[lax.rem(step, 2)],
             recv_sem=recv_sem.at[lax.rem(step, 2), group],
             device_id=targets[j],
             device_id_type=MESH,
@@ -190,16 +189,13 @@
         for j in which:
             send(step, group, j).start()
 
-    def wait_all(buf, sems, step, group):
-        parts = buf.at[step, :, pl.ds(group * k_group, k_group), :]
-        pltpu.make_async_copy(parts, parts, sems.at[lax.rem(step, 2), group]).wait()
-
     def wait_recvs(step, group):
-        wait_all(recv_buf, recv_sem, step, group)
+        parts = recv_buf.at[step, :, pl.ds(group * k_group, k_group), :]
+        pltpu.make_async_copy(parts, parts, recv_sem.at[lax.rem(step, 2), group]).wait()
 
     def wait_sends(step):
-        for group in range(groups):
-            wait_all(send_buf, send_sem, step, group)
+        whole = send_buf.at[step]
+        pltpu.make_async_copy(whole, whole, send_sem.at[lax.rem(step, 2)]).wait()
 
     for group in range(groups):
         at = slice(group * k_group, (group + 1) * k_group)
@@ -309,8 +305,8 @@
         return [pltpu.matmul_pop(top) + pltpu.matmul_pop(bottom) for top, bottom in field_accs]
 
     on_own = jnp.concatenate([diag[b : b + 1, :] for b in range(blk_rows)], axis=1)
-    line = lax.broadcasted_iota(jnp.int32, (2 * k_group, rows), 0)
-    rest, thirds = on_own, jnp.zeros((2 * k_group, rows), f32)
+    line = lax.broadcasted_iota(jnp.int32, (k_group, rows), 0)
+    rest, thirds = on_own, jnp.zeros((k_group, rows), f32)
     for i in range(3):
         third = rest.astype(jnp.bfloat16).astype(f32)
         thirds = jnp.where(line == i, third, thirds)
@@ -346,17 +342,17 @@
                 tile_cols = slice(first_col + half * CUT, first_col + (half + 1) * CUT)
                 pltpu.matmul_push_rhs(weights[tile_rows, tile_cols], staging_register=i, mxu_index=u)
 
-    def multiply(parts, half, slot):
-        for i in range(2):
+    def multiply(high, low, half, slot):
+        for operand, part_of, load in ((high, 0, 0), (low, 1, None), (high, 0, 1)):
             for u in units:
-                acc = halo_accs[u][2 * slot + half]
-                pltpu.matmul_acc_lhs(acc, parts[:, u * CUT : (u + 1) * CUT], load_staged_rhs=i)
+                acc = halo_accs[u][4 * slot + 2 * half + part_of]
+                pltpu.matmul_acc_lhs(acc, operand[:, u * CUT : (u + 1) * CUT], load_staged_rhs=load)
 
     def collect(half, slot):
-        both = pltpu.matmul_pop(halo_accs[0][2 * slot + half])
-        for u in units[1:]:
-            both = both + pltpu.matmul_pop(halo_accs[u][2 * slot + half])
-        return both[:k_group] + both[k_group:]
+        i = 4 * slot + 2 * half
+        return sum(pltpu.matmul_pop(halo_accs[u][i + 1]) for u in units) + sum(
+            pltpu.matmul_pop(halo_accs[u][i]) for u in units
+        )
 
     def iteration(step, carry):
         alpha = coef[2 * step][0:1]
@@ -366,15 +362,18 @@
         def finish(group, half):
             at = slice(group * k_group, (group + 1) * k_group)
             lanes = slice(half * CUT, (half + 1) * CUT)
-            r_new = r_pack[at, lanes] - (part[at, lanes] + collect(half, group % 2))
-            d_new = alpha[:, lanes] * d_pack[at, lanes] + beta[:, lanes] * r_new
+            r_part = r_pack[at, lanes] - part[at, lanes]
+            d_part = alpha[:, lanes] * d_pack[at, lanes] + beta[:, lanes] * r_part
             x_old = x_pack[at, lanes]
-            going = d_new + last * x_old
+            coupled = collect(half, group % 2)
+            change = beta[:, lanes] * coupled
+            going = (d_part + last * x_old) - change
             which = range(half * CUT // tile, (half + 1) * CUT // tile)
             for i, j in enumerate(which):
                 send_buf[step + 1, j, at, :] = going[:, i * tile : (i + 1) * tile]
             start_sends(step + 1, group, which)
-            r_pack[at, lanes] = r_new
+            d_new = d_part - change
+            r_pack[at, lanes] = r_part - coupled
             d_pack[at, lanes] = d_new
             x_pack[at, lanes] = x_old + d_new
 
@@ -382,10 +381,9 @@
         for group in range(groups):
             g0 = group * k_group
             high, low = take_halo(step, group)
-            parts = jnp.concatenate([high, low], axis=0)
-            multiply(parts, 0, group % 2)
+            multiply(high, low, 0, group % 2)
             stage(rows, 1)
-            multiply(parts, 1, group % 2)
+            multiply(high, low, 1, group % 2)
             if group + 1 < groups:
                 stage(rows, 0)
             finish(group, 0)
@@ -420,7 +418,7 @@
     for i in range(blk_rows):
         out_buf[i * tile : (i + 1) * tile, :] = jnp.transpose(x_own[:, i * tile : (i + 1) * tile])
 
-    out_copy = pltpu.make_async_copy(out_buf, x_out, out_sem)
+    out_copy = pltpu.make_async_copy(out_buf, x_out, copy_sems.at[5])
     out_copy.start()
     pl.semaphore_wait(hello_sems.at[1], 2)
 
@@ -438,10 +436,9 @@
     stage(0, 0)
     for group in range(groups):
         high, low = take_halo(ITERS - 1, group)
-        parts = jnp.concatenate([high, low], axis=0)
-        multiply(parts, 0, group % 2)
+        multiply(high, low, 0, group % 2)
         stage(0, 1)
-        multiply(parts, 1, group % 2)
+        multiply(high, low, 1, group % 2)
         if group > 0:
             squares.append(square(group - 1))
         if group + 1 < groups:
@@ -456,8 +453,8 @@
         pltpu.make_async_remote_copy(
             src_ref=plane_send,
             dst_ref=plane_recv.at[my_slot],
-            send_sem=norm_sems.at[0],
-            recv_sem=norm_sems.at[1],
+            send_sem=copy_sems.at[0],
+            recv_sem=norm_sems.at[0],
             device_id=plane_target(step),
             device_id_type=MESH,
         )
@@ -466,18 +463,18 @@
     for copy in plane_copies:
         copy.start()
     others = plane_recv.at[pl.ds(0, in_plane - 1)]
-    pltpu.make_async_copy(others, others, norm_sems.at[1]).wait()
+    pltpu.make_async_copy(others, others, norm_sems.at[0]).wait()
     mine = jnp.sum(plane_recv[...], axis=0)
 
     axis_send[...] = mine
-    own_copy = pltpu.make_async_copy(axis_send, axis_recv.at[my_plane], norm_sems.at[4])
+    own_copy = pltpu.make_async_copy(axis_send, axis_recv.at[my_plane], copy_sems.at[4])
     own_copy.start()
     axis_copies = [
         pltpu.make_async_remote_copy(
             src_ref=axis_send,
             dst_ref=axis_recv.at[my_plane],
-            send_sem=norm_sems.at[2],
-            recv_sem=norm_sems.at[3],
+            send_sem=copy_sems.at[2],
+            recv_sem=norm_sems.at[1],
             device_id=axis_target(offset),
             device_id_type=MESH,
         )
@@ -487,15 +484,15 @@
         copy.start()
     wait_sends(ITERS - 1)
     out_copy.wait()
-    pltpu.make_async_copy(others, others, norm_sems.at[0]).wait()
+    pltpu.make_async_copy(others, others, copy_sems.at[0]).wait()
     others = axis_recv.at[pl.ds(0, planes - 1)]
-    pltpu.make_async_copy(others, others, norm_sems.at[3]).wait()
+    pltpu.make_async_copy(others, others, norm_sems.at[1]).wait()
     own_copy.wait()
-    pltpu.make_async_copy(others, others, norm_sems.at[2]).wait()
+    pltpu.make_async_copy(others, others, copy_sems.at[2]).wait()
 
 
 def kernel(shape, groups, k_all, rows, *refs):
-    heights = (CUT, CUT, k_all, k_all) + 4 * (2 * k_all // groups,)
+    heights = (CUT, CUT, k_all, k_all) + 8 * (k_all // groups,)
     units = rows // CUT
     specs = [pltpu.ACC(unit)((height, CUT), jnp.float32) for unit in range(units) for height in heights]
 
@@ -550,11 +547,10 @@
             pltpu.VMEM((in_plane, 1, k_all), f32),
             pltpu.VMEM((1, k_all), f32),
             pltpu.SemaphoreType.DMA((7,)),
+            pltpu.SemaphoreType.DMA((2,)),
             pltpu.SemaphoreType.DMA((2, GROUPS)),
-            pltpu.SemaphoreType.DMA((2, GROUPS)),
-            pltpu.SemaphoreType.DMA((5,)),
+            pltpu.SemaphoreType.DMA((2,)),
             pltpu.VMEM((rows, k_all), f32),
-            pltpu.SemaphoreType.DMA,
             pltpu.SemaphoreType.REGULAR((2,)),
             pltpu.VMEM((8, rows), f32),
         ],

time: 53.1 us -> 52.9 us (level)
  no operation moved by 1% of the time
where the time goes in v8:
time: 52.9 us; the launch traced here: 52.7 us
  Pallas kernels  52.1 us (98%)
  between operations  0.64 us (1%)
    pallas_call x1, Pallas kernels, on_device(): pl.pallas_call(functools.partial(kernel, (n_patch, n_sub, planes), GROUPS...  50.4 us
    pallas_call x1, Pallas kernels, settle(): pl.pallas_call(settle_kernel, out_shape=(jax.ShapeDtypeStruct(x.shape, x....  1.67 us

profile of v8, /device:TPU:1, one launch (start us, length us, event | category | flops | bytes accessed | tf_op | source)
XLA Modules:
  0.0 52.7 jit_solution(4279650797246729837)
XLA Ops:
  0.6 50.4 %shard_map.86 = (f32[512,128]{1,0:T(8,128)}, f32[8,1,128]{2,1,0:T(1,128)}) custom-call(s32[16,128]{1,0:T(8,128)} %bitcast.4, f32[4,128]{1,0:T(4,128)} %bitcast.5, s32[4,6]{1,0:T(4,128)} %refs_2_.1, s32[4,128]{1,0:T(4,128)} %bitcast.6, s32[1,512]{1,0:T(1,128)} %refs_4_.1, f32[2]{0:T(128)} %refs_5_.1, f32[4,6,128,128]{3,2,1,0:T(8,128)} %refs_6_.1), custom_call_target="tpu_custom_call" | custom-call | tf_op jit(solution)/shard_map/pallas_call | solution.py:516
  51.1 1.7 %shard_map.87 = (f32[512,128]{1,0:T(8,128)}, f32[1,128]{1,0:T(1,128)}) custom-call(f32[512,128]{1,0:T(8,128)} %get-tuple-element.6.x_in, f32[8,1,128]{2,1,0:T(1,128)} %get-tuple-element.7.sums_in), custom_call_target="tpu_custom_call" | custom-call | tf_op jit(solution)/shard_map/pallas_call | solution.py:591

commit v9 on v8

--- a/solution.py
+++ b/solution.py
@@ -135,11 +135,14 @@
             )
         )
     ]
+    barrier = pltpu.get_barrier_semaphore()
+    greeted = 0
+    for target in targets[:2]:
+        pl.semaphore_signal(barrier, inc=1, device_id=target, device_id_type=MESH)
+        greeted += 1
     for load in loads:
         load.start()
-    barrier = pltpu.get_barrier_semaphore()
-    greeted = 0
-    for target in targets:
+    for target in targets[2:]:
         pl.semaphore_signal(barrier, inc=1, device_id=target, device_id_type=MESH)
         greeted += 1
     for offset in (1, planes - 1):
@@ -464,7 +467,10 @@
         copy.start()
     others = plane_recv.at[pl.ds(0, in_plane - 1)]
     pltpu.make_async_copy(others, others, norm_sems.at[0]).wait()
-    mine = jnp.sum(plane_recv[...], axis=0)
+    sums = [plane_recv[i] for i in range(in_plane)]
+    while len(sums) > 1:
+        sums = [sum(sums[i : i + 2]) for i in range(0, len(sums), 2)]
+    mine = sums[0]
 
     axis_send[...] = mine
     own_copy = pltpu.make_async_copy(axis_send, axis_recv.at[my_plane], copy_sems.at[4])

time: 52.9 us -> 52.9 us (level)
  no operation moved by 1% of the time
where the time goes in v9:
time: 52.9 us; the launch traced here: 52.7 us
  Pallas kernels  52.1 us (98%)
  between operations  0.64 us (1%)
    pallas_call x1, Pallas kernels, on_device(): pl.pallas_call(functools.partial(kernel, (n_patch, n_sub, planes), GROUPS...  50.4 us
    pallas_call x1, Pallas kernels, settle(): pl.pallas_call(settle_kernel, out_shape=(jax.ShapeDtypeStruct(x.shape, x....  1.67 us

profile of v9, /device:TPU:1, one launch (start us, length us, event | category | flops | bytes accessed | tf_op | source)
XLA Modules:
  0.0 52.7 jit_solution(9024597404498705707)
XLA Ops:
  0.6 50.4 %shard_map.86 = (f32[512,128]{1,0:T(8,128)}, f32[8,1,128]{2,1,0:T(1,128)}) custom-call(s32[16,128]{1,0:T(8,128)} %bitcast.4, f32[4,128]{1,0:T(4,128)} %bitcast.5, s32[4,6]{1,0:T(4,128)} %refs_2_.1, s32[4,128]{1,0:T(4,128)} %bitcast.6, s32[1,512]{1,0:T(1,128)} %refs_4_.1, f32[2]{0:T(128)} %refs_5_.1, f32[4,6,128,128]{3,2,1,0:T(8,128)} %refs_6_.1), custom_call_target="tpu_custom_call" | custom-call | tf_op jit(solution)/shard_map/pallas_call | solution.py:522
  51.1 1.7 %shard_map.87 = (f32[512,128]{1,0:T(8,128)}, f32[1,128]{1,0:T(1,128)}) custom-call(f32[512,128]{1,0:T(8,128)} %get-tuple-element.6.x_in, f32[8,1,128]{2,1,0:T(1,128)} %get-tuple-element.7.sums_in), custom_call_target="tpu_custom_call" | custom-call | tf_op jit(solution)/shard_map/pallas_call | solution.py:597
